TPU v7x, 8 devices: a whole 2x2x1 slice. The times are simulated.
8 devices in a mesh: dp: 1 (over z), sp: 8 (over y, x, core).
Axes of the slice: x: 2, y: 2, z: 1, core: 2. Of those that a mesh axis runs over, the one named last changes fastest.
Arguments:
- x: bfloat16 [16, 1024, 2048], P('dp', 'sp')
- g: bfloat16 [16, 1024, 2048], P('dp', 'sp')
- ln_g: float32 [2048], replicated
- ln_b: float32 [2048], replicated
- w_qkv: bfloat16 [2048, 3, 32, 64], replicated
- b_qkv: float32 [3, 32, 64], replicated
- w_out: bfloat16 [32, 64, 2048], replicated
- b_out: float32 [2048], replicated
Outputs:
- output 1: bfloat16 [16, 1024, 2048], P('dp', 'sp')
- output 2: bfloat16 [16, 1024, 2048], P('dp', 'sp')
- output 3: float32 [2048], P('dp')
- output 4: float32 [2048], P('dp')
- output 5: float32 [2048, 3, 32, 64], P('dp')
- output 6: float32 [3, 32, 64], P('dp')
- output 7: float32 [32, 64, 2048], P('dp')
- output 8: float32 [2048], P('dp')
All inputs are finite; a program needn't handle non-finite values.
Results may differ from a plain program's by a relative error of at most 0.00839964.
Values are sent between devices in bfloat16 or wider.
A program may use at most 1 GiB of HBM per device.

v0:
```python
import jax
import jax.numpy as jnp
from jax import lax
from jax.experimental import pallas as pl
from jax.experimental.pallas import tpu as pltpu
from jax.sharding import Mesh, PartitionSpec as P

LN_EPS = 1e-5
LOG2E = 1.4426950408889634
F32, BF16 = jnp.float32, jnp.bfloat16
NN = (((1,), (0,)), ((), ()))
NT = (((1,), (1,)), ((), ()))
RUN, BATCH, MODEL, HEADS, HEAD = 128, 2, 2048, 32, 64
SHARDS = 8
SEQ = SHARDS * RUN
TOKENS = SEQ * BATCH
PAIRS = HEADS // 2
LATE = 2
EARLY = PAIRS - LATE
SENDS = 8
LANES = 2 * HEAD
HALF = MODEL // 2
MESH = pl.DeviceIdType.MESH
AXES = ('y', 'x', 'core')
DMA = pltpu.SemaphoreType.DMA


class Place:
    def __init__(self):
        self.y, self.x, self.core = (lax.axis_index(n) for n in AXES)
        y, x, core = self.y, self.x, self.core
        self.me = y * 4 + x * 2 + core
        self.c1 = (1 - core) * x + core * y
        self.c2 = (1 - core) * y + core * x
        self.n1 = (0, y + core * (1 - 2 * y), x + (1 - core) * (1 - 2 * x), core)
        self.n2 = (0, y + (1 - core) * (1 - 2 * y), x + core * (1 - 2 * x), core)
        self.mate = (0, y, x, 1 - core)

    def peer(self, u):
        fc, fy, fx = u // 4, (u // 2) % 2, u % 2
        flip = lambda v, f: v + f * (1 - 2 * v)
        return flip(self.y, fy), flip(self.x, fx), flip(self.core, fc)

    def slot(self, run):
        flip = lambda v, f: v + f * (1 - 2 * v)
        return flip(self.core, run % 2) * 4 + flip(self.y, run // 4) * 2 + flip(self.x, (run // 2) % 2)

    def meet_all(self):
        barrier = pltpu.get_barrier_semaphore()
        for u in range(1, SHARDS):
            pl.semaphore_signal(barrier, inc=1, device_id=(0,) + self.peer(u), device_id_type=MESH)
        pl.semaphore_wait(barrier, SHARDS - 1)


def remote(src, dst, send, recv, to):
    return pltpu.make_async_remote_copy(src, dst, send, recv, device_id=to, device_id_type=MESH)


class Reduce:
    def __init__(self, at, out_ref, base, part, recv1, recv2, sems):
        self.at, self.out, self.base = at, out_ref, base
        self.part, self.recv1, self.recv2 = part, recv1, recv2
        (self.rs1_s, self.rs1_r, self.rs2_s, self.rs2_r, self.ag_s, self.n1_r, self.n2_r, self.fw_r,
         self.fw_s, self.core_s, self.core_r) = sems
        self.cols = pl.ds(pl.multiple_of(at.core * HALF, HALF), HALF)

    def piece(self, t, k):
        return self.out.at[t, self.base + k, :, self.cols]

    def rs1(self, k):
        s = k % 2
        return remote(self.part.at[s, pl.ds((1 - self.at.c1) * 2, 2)], self.recv1.at[s],
                      self.rs1_s.at[s], self.rs1_r.at[s], self.at.n1)

    def rs2(self, k):
        s = k % 2
        return remote(self.part.at[s, self.at.c1 * 2 + 1 - self.at.c2], self.recv2.at[s],
                      self.rs2_s.at[s], self.rs2_r.at[s], self.at.n2)

    def own(self, k):
        s, t = k % 2, self.at.c1 * 2 + self.at.c2
        src, dst = self.part.at[s, t], self.piece(t, k)
        return (remote(src, dst, self.ag_s.at[s, 0], self.n1_r.at[s], self.at.n1),
                remote(src, dst, self.ag_s.at[s, 1], self.n2_r.at[s], self.at.n2),
                remote(src, dst, self.ag_s.at[s, 2], self.core_r, self.at.mate),
                pltpu.make_async_copy(src, dst, self.ag_s.at[s, 3]))

    def to_mate(self, t, k):
        at = self.piece(t, k)
        remote(at, at, self.core_s, self.core_r, self.at.mate).start()

    def arrived(self, t, k, sem):
        pltpu.make_async_copy(self.piece(t, k), self.piece(t, k), sem).wait()

    def scatter1(self, k):
        self.rs1(k).start()

    def scatter2(self, k):
        s, keep = k % 2, pl.ds(self.at.c1 * 2, 2)
        self.rs1(k).wait()
        self.part[s, keep] = self.part[s, keep] + self.recv1[s]
        self.rs2(k).start()

    def gather(self, k):
        s, t = k % 2, self.at.c1 * 2 + self.at.c2
        self.rs2(k).wait()
        self.part[s, t] = self.part[s, t] + self.recv2[s]
        for copy in self.own(k):
            copy.start()

    def forward(self, k):
        s = k % 2
        t_n2, t_n1 = self.at.c1 * 2 + 1 - self.at.c2, (1 - self.at.c1) * 2 + self.at.c2
        self.arrived(t_n2, k, self.n2_r.at[s])
        at = self.piece(t_n2, k)
        remote(at, at, self.fw_s, self.fw_r.at[s], self.at.n1).start()
        self.to_mate(t_n2, k)
        self.arrived(t_n1, k, self.n1_r.at[s])
        self.to_mate(t_n1, k)

    def last(self, k):
        t = (1 - self.at.c1) * 2 + 1 - self.at.c2
        self.arrived(t, k, self.fw_r.at[k % 2])
        self.to_mate(t, k)

    def own_sent(self, k):
        *sent, kept = self.own(k)
        for copy in sent:
            copy.wait_send()
        kept.wait()

    def finish(self, count):
        rows = pl.ds(self.base, count)
        half = pl.ds(0, HALF)
        for ref, sem in ((self.out.at[:, rows, :, half], self.core_r), (self.out.at[0:3, rows, :, half], self.core_s),
                         (self.out.at[0, rows, :, half], self.fw_s)):
            pltpu.make_async_copy(ref, ref, sem).wait()


REDUCE_SCRATCH = [
    pltpu.VMEM((2, 4, LANES, HALF), F32), pltpu.VMEM((2, 2, LANES, HALF), F32), pltpu.VMEM((2, LANES, HALF), F32),
    DMA((2,)), DMA((2,)), DMA((2,)), DMA((2,)), DMA((2, 4)), DMA((2,)), DMA((2,)), DMA((2,)), DMA, DMA, DMA]


def fold(v, op):
    r = v[0:8]
    for t in range(8, v.shape[0], 8):
        r = op(r, v[t:t + 8])
    return r


def attend(b, slots, q, k, v, da, a_ref, dq_ref, dk_ref, dv_ref, kt, vt, dk_acc, dv_acc):
    first = lax.broadcasted_iota(jnp.int32, (SEQ, LANES), 1) < HEAD
    zero = jnp.zeros_like(q)
    qm = (jnp.where(first, q, zero), jnp.where(first, zero, q))
    dm = (jnp.where(first, da, zero), jnp.where(first, zero, da))
    kt[...] = k.T
    vt[...] = v.T
    blk, ch = 256, 128
    scale = HEAD ** -0.5
    cc = scale * LOG2E
    dot = lambda l, r, dims=NN: lax.dot_general(l, r, dims, preferred_element_type=F32)

    def scores(i):
        ext, qs = (i + 1) * blk, slice(i * blk, (i + 1) * blk)
        return [(dot(k[:ext], qm[h][qs], NT), dot(v[:ext], dm[h][qs], NT)) for h in range(2)]

    def softmax(i, pair):
        ext = (i + 1) * blk
        s, dp = ([m[t:t + ch] for t in range(0, ext, ch)] for m in pair)
        top = total = cross = None
        for n, t in enumerate(range(0, ext, ch)):
            if t >= i * blk:
                rows = lax.broadcasted_iota(jnp.int32, (ch, blk), 0) + (t - i * blk)
                s[n] = jnp.where(rows <= lax.broadcasted_iota(jnp.int32, (ch, blk), 1), s[n], -jnp.inf)
            f = fold(s[n], jnp.maximum)
            top = f if top is None else jnp.maximum(top, f)
        top = jnp.max(top, axis=0, keepdims=True) * cc
        for n in range(len(s)):
            s[n] = jnp.exp2(s[n] * cc - top)
            f, fx = fold(s[n], jnp.add), fold(s[n] * dp[n], jnp.add)
            total = f if total is None else total + f
            cross = fx if cross is None else cross + fx
        inv = 1.0 / jnp.sum(total, axis=0, keepdims=True)
        c = jnp.sum(cross, axis=0, keepdims=True) * inv
        pb, ds = [], []
        for n in range(len(s)):
            p = s[n] * inv
            pb.append(p.astype(BF16))
            ds.append((p * (dp[n] - c)).astype(BF16))
        return jnp.concatenate(pb, axis=0), jnp.concatenate(ds, axis=0)

    def outputs(i, pd):
        old, ext = i * blk, (i + 1) * blk
        qs = slice(old, ext)
        both = lambda m: jnp.concatenate([m[0][qs], m[1][qs]], axis=0)
        halves = [slice(0, HEAD), slice(HEAD, LANES)]
        o = jnp.concatenate([dot(vt[halves[h], :ext], pd[h][0]) for h in range(2)], axis=0)
        dq = jnp.concatenate([dot(kt[halves[h], :ext], pd[h][1]) for h in range(2)], axis=0)
        dv = dot(jnp.concatenate([pd[0][0], pd[1][0]], axis=1), both(dm))
        dk = dot(jnp.concatenate([pd[0][1], pd[1][1]], axis=1), both(qm))
        if old:
            dv_acc[:old] += dv[:old]
            dk_acc[:old] += dk[:old]
        dv_acc[old:ext] = dv[old:]
        dk_acc[old:ext] = dk[old:]
        o, dq = o.T.astype(BF16), (dq.T * scale).astype(BF16)
        for r in range(2):
            a_ref[slots[2 * i + r], b] = o[r * RUN:(r + 1) * RUN]
            dq_ref[slots[2 * i + r], b] = dq[r * RUN:(r + 1) * RUN]

    count = SEQ // blk
    ready = scores(0)
    for i in range(count):
        pd = [softmax(i, ready[h]) for h in range(2)]
        if i + 1 < count:
            ready = scores(i + 1)
        outputs(i, pd)
    for r in range(SHARDS):
        run = slice(r * RUN, (r + 1) * RUN)
        dk_ref[slots[r], b] = (dk_acc[run] * scale).astype(BF16)
        dv_ref[slots[r], b] = dv_acc[run].astype(BF16)


def pairs_kernel(x_ref, g_ref, lg_ref, lb_ref, w_ref, wo_ref, b_ref,
                 out_ref, xt_ref, gt_ref, late_ref, a_ref, dq_ref, dk_ref, dv_ref, small_ref,
                 h, g, qkv, da, lhs_t, kt, vt, dk_acc, dv_acc, away, met,
                 x_s, x_r, g_s, g_r, keep_s, late_s, met_s, met_r, part, recv1, recv2, *sems):
    j = pl.program_id(0)
    par = j % 2
    at = Place()
    red = Reduce(at, out_ref, 0, part, recv1, recv2, sems)
    slots = [at.slot(r) for r in range(SHARDS)]

    def send_x(u):
        py, px, pc = at.peer(u)
        rows = x_ref.at[pl.ds((py * 4 + px * 2 + pc) * BATCH, BATCH)]
        if u == 0:
            return pltpu.make_async_copy(rows, h.at[0], x_r.at[0])
        return remote(rows, h.at[u], x_s.at[u], x_r.at[u], (0, py, px, pc))

    def send_g(b, u):
        py, px, pc = at.peer(u)
        row = g_ref.at[(py * 4 + px * 2 + pc) * BATCH + b]
        if u == 0:
            return pltpu.make_async_copy(row, g.at[0, b], g_r.at[b, 0])
        return remote(row, g.at[u, b], g_s.at[b, u], g_r.at[b, u], (0, py, px, pc))

    def g_landed(b, u):
        pltpu.make_async_copy(g.at[u, b], g.at[u, b], g_r.at[b, u]).wait()

    @pl.when(j == 0)
    def _():
        at.meet_all()
        order = (0, 3, 1, 2, 7, 5, 6, 4)
        for u in order:
            send_x(u).start()
        for b in range(BATCH):
            for u in order:
                send_g(b, u).start()
        for u in (0, 4, 1, 2, 3, 5, 6, 7):
            pltpu.make_async_copy(h.at[u], h.at[u], x_r.at[u]).wait()
            out = pltpu.make_async_copy(h.at[u], xt_ref.at[u], keep_s)
            out.start()
            out.wait()
            for b in range(BATCH):
                xf = h[u, b].astype(F32)
                cen = xf - jnp.mean(xf, axis=-1, keepdims=True)
                inv = lax.rsqrt(jnp.mean(cen * cen, axis=-1, keepdims=True) + LN_EPS)
                h[u, b] = ((cen * inv) * lg_ref[...] + lb_ref[...]).astype(BF16)

    @pl.when(par == 0)
    def _():
        w = w_ref[...].reshape(6 * LANES, MODEL)
        step = 4
        for r in range(0, SHARDS, step):
            hr = h[r:r + step].reshape(step * BATCH * RUN, MODEL)
            res = (lax.dot_general(hr, w, NT, preferred_element_type=F32) + b_ref[0]).astype(BF16)
            for t in range(6):
                qkv[t, r:r + step] = res[:, t * LANES:(t + 1) * LANES].reshape(step, BATCH, RUN, LANES)

    def project_da(b):
        res = lax.dot_general(g[:, b].reshape(SEQ, MODEL), wo_ref[...].reshape(2 * LANES, MODEL), NT,
                              preferred_element_type=F32).astype(BF16)
        for t in range(2):
            da[t, :, b] = res[:, t * LANES:(t + 1) * LANES].reshape(SHARDS, RUN, LANES)

    def one(b):
        gathered = lambda ref, t: jnp.concatenate([ref[t, slots[r], b] for r in range(SHARDS)], axis=0)
        cols = [gathered(qkv, 2 * t + par) for t in range(3)]
        attend(b, slots, *cols, gathered(da, par), a_ref, dq_ref, dk_ref, dv_ref, kt, vt, dk_acc, dv_acc)

    @pl.when(j >= 2)
    def _():
        red.gather(j - 2)

    @pl.when(j == 0)
    def _():
        for u in range(SHARDS):
            g_landed(0, u)

    @pl.when(par == 0)
    def _():
        project_da(0)

    one(0)

    @pl.when(j == 0)
    def _():
        for u in range(SHARDS):
            g_landed(1, u)
        pltpu.make_async_copy(g, gt_ref, keep_s).start()

    @pl.when(par == 0)
    def _():
        project_da(1)

    one(1)

    @pl.when(j >= 2)
    def _():
        red.forward(j - 2)

    at_pair = pl.ds(pl.multiple_of(j * LANES, LANES), LANES)
    for t, ref in enumerate((dq_ref, dk_ref, dv_ref, a_ref)):
        d = ref[...].reshape(TOKENS, LANES)
        lhs_t[t * LANES:(t + 1) * LANES] = d.T
        if t < 3:
            small_ref[t:t + 1, at_pair] = jnp.sum(d.astype(F32), axis=0, keepdims=True)

    @pl.when(j == 1)
    def _():
        for u in range(1, SHARDS):
            send_x(u).wait_send()
            for b in range(BATCH):
                send_g(b, u).wait_send()
        pltpu.make_async_copy(g, gt_ref, keep_s).wait()
        total = jnp.zeros((1, MODEL), F32)
        for u in range(SHARDS):
            total += jnp.sum(g[u].reshape(BATCH * RUN, MODEL).astype(F32), axis=0, keepdims=True)
        small_ref[3:4] = total
        small_ref[4:8] = jnp.zeros((4, MODEL), F32)

    def weight_grad(dst, start):
        for t in range(0, HALF, 512):
            cols = pl.ds(pl.multiple_of(start + t, 512), 512)
            hc = h[:, :, :, cols].reshape(TOKENS, 512)
            gc = g[:, :, :, cols].reshape(TOKENS, 512)
            r = lax.dot_general(lhs_t[0:3 * LANES], hc, NN, preferred_element_type=F32)
            dst[0:3, :, t:t + 512] = r.reshape(3, LANES, 512)
            dst[3, :, t:t + 512] = lax.dot_general(lhs_t[3 * LANES:], gc, NN, preferred_element_type=F32)

    def meet(k):
        return remote(away, met.at[k % 2], met_s, met_r.at[k % 2], at.mate)

    @pl.when(j >= 1)
    def _():
        meet(j - 1).wait_send()
    weight_grad(away, (1 - at.core) * HALF)
    meet(j).start()

    @pl.when((j >= 1) & (j <= EARLY))
    def _():
        red.scatter2(j - 1)

    @pl.when(j >= 2)
    def _():
        red.own_sent(j - 2)
    weight_grad(part.at[par], at.core * HALF)

    @pl.when(j >= 2)
    def _():
        red.last(j - 2)
    meet(j).wait_recv()
    part[par] = part[par] + met[par]

    @pl.when(j < EARLY)
    def _():
        red.scatter1(j)

    @pl.when(j >= EARLY)
    def _():
        pltpu.make_async_copy(part.at[par], late_ref.at[j - EARLY], late_s.at[par]).start()

    @pl.when(j == PAIRS - 1)
    def _():
        meet(PAIRS - 1).wait_send()
        for k in range(LATE):
            pltpu.make_async_copy(part.at[k], late_ref.at[k], late_s.at[k]).wait()
        red.finish(EARLY)


def head_pairs(x, g, ln_g, ln_b, w_rows, wo_rows, bias):
    hbm = pl.BlockSpec(memory_space=pl.ANY)
    vec = pl.BlockSpec((1, MODEL), lambda j: (0, 0))
    col = pl.BlockSpec((SHARDS, BATCH, RUN, LANES), lambda j: (0, 0, 0, j))
    runs = (SHARDS, BATCH, RUN, MODEL)
    return pl.pallas_call(
        pairs_kernel, grid=(PAIRS,),
        in_specs=[hbm, hbm, vec, vec, pl.BlockSpec((3, 2, LANES, MODEL), lambda j: (0, j // 2, 0, 0)),
                  pl.BlockSpec((2, LANES, MODEL), lambda j: (j // 2, 0, 0)),
                  pl.BlockSpec((1, 1, 6 * LANES), lambda j: (j // 2, 0, 0))],
        out_specs=[hbm, hbm, hbm, hbm, col, col, col, col, pl.BlockSpec((8, MODEL), lambda j: (0, 0))],
        out_shape=[jax.ShapeDtypeStruct((4, PAIRS, LANES, MODEL), F32), jax.ShapeDtypeStruct(runs, BF16),
                   jax.ShapeDtypeStruct(runs, BF16), jax.ShapeDtypeStruct((LATE, 4, LANES, HALF), F32)]
        + [jax.ShapeDtypeStruct(runs, BF16)] * 4 + [jax.ShapeDtypeStruct((8, MODEL), F32)],
        scratch_shapes=[
            pltpu.VMEM(runs, BF16), pltpu.VMEM(runs, BF16),
            pltpu.VMEM((6, SHARDS, BATCH, RUN, LANES), BF16), pltpu.VMEM((2, SHARDS, BATCH, RUN, LANES), BF16),
            pltpu.VMEM((4 * LANES, TOKENS), BF16),
            pltpu.VMEM((LANES, SEQ), BF16), pltpu.VMEM((LANES, SEQ), BF16),
            pltpu.VMEM((SEQ, LANES), F32), pltpu.VMEM((SEQ, LANES), F32),
            pltpu.VMEM((4, LANES, HALF), F32), pltpu.VMEM((2, 4, LANES, HALF), F32),
            DMA((SHARDS,)), DMA((SHARDS,)), DMA((BATCH, SHARDS)), DMA((BATCH, SHARDS)), DMA, DMA((2,)), DMA, DMA((2,))]
        + REDUCE_SCRATCH,
        name="head_pairs",
        compiler_params=pltpu.CompilerParams(collective_id=0, has_side_effects=True, vmem_limit_bytes=63 << 20),
        cost_estimate=pl.CostEstimate(flops=500_000_000_000, transcendentals=0, bytes_accessed=100 << 20),
    )(x, g, ln_g.reshape(1, MODEL), ln_b.reshape(1, MODEL), w_rows, wo_rows, bias)


def tokens_kernel(w_ref, wo_ref, late_ref, grads_ref, small_ref, lg_ref, bo_ref,
                  a_ref, dq_ref, dk_ref, dv_ref, x_ref, g_ref,
                  out_ref, y_ref, dx_ref, sum_ref,
                  w, wo, ybuf, dxbuf, smalls,
                  w_s, wo_s, late_s, y_s, y_r, dx_s, sm_s, sm_r, part, recv1, recv2, *sems):
    i = pl.program_id(0)
    at = Place()
    red = Reduce(at, out_ref, EARLY, part, recv1, recv2, sems)
    u, b = SHARDS - 1 - i // BATCH, i % BATCH
    py, px, pc = at.peer(u)
    peer = py * 4 + px * 2 + pc
    get_w = pltpu.make_async_copy(w_ref, w, w_s)
    get_wo = pltpu.make_async_copy(wo_ref, wo, wo_s)

    def late(k):
        return pltpu.make_async_copy(late_ref.at[k], part.at[k], late_s.at[k])

    @pl.when(i == 0)
    def _():
        for k in range(LATE):
            late(k).start()
        get_wo.start()
        get_w.start()
        at.meet_all()
        for k in range(LATE):
            late(k).wait()
            red.scatter1(k)
        smalls[0] = small_ref[...]
        get_wo.wait()

    for step, tick, k in ((3, red.scatter2, 0), (4, red.scatter2, 1), (7, red.gather, 0), (9, red.gather, 1),
                          (10, red.forward, 0), (12, red.forward, 1), (13, red.last, 0)):
        @pl.when(i == step)
        def _(tick=tick, k=k):
            tick(k)

    s = i % SENDS
    row = at.me * BATCH + b

    def y_out(slot):
        return remote(ybuf.at[slot], y_ref.at[row], y_s.at[slot], y_r, (0, py, px, pc))

    def y_kept(slot):
        return pltpu.make_async_copy(ybuf.at[slot], y_ref.at[row], y_s.at[slot])

    @pl.when(i >= SENDS)
    def _():
        y_out(s).wait_send()
    acc = jnp.dot(a_ref[0, 0], wo[...], preferred_element_type=F32)
    x = x_ref[0, 0].astype(F32)
    ybuf[s] = (x + acc + bo_ref[...]).astype(BF16)

    @pl.when(i < BATCH * (SHARDS - 1))
    def _():
        y_out(s).start()

    @pl.when(i >= BATCH * (SHARDS - 1))
    def _():
        y_kept(s).start()

    @pl.when(i == 0)
    def _():
        get_w.wait()
    dh = jnp.dot(dq_ref[0, 0], w[0:MODEL], preferred_element_type=F32)
    dh += jnp.dot(dk_ref[0, 0], w[MODEL:2 * MODEL], preferred_element_type=F32)
    dh += jnp.dot(dv_ref[0, 0], w[2 * MODEL:], preferred_element_type=F32)
    cen = x - jnp.mean(x, axis=-1, keepdims=True)
    inv = lax.rsqrt(jnp.mean(cen * cen, axis=-1, keepdims=True) + LN_EPS)
    xn = cen * inv
    smalls[0, 4:5] += jnp.sum(dh * xn, axis=0, keepdims=True)
    smalls[0, 5:6] += jnp.sum(dh, axis=0, keepdims=True)
    v = dh * lg_ref[...]
    dv = inv * (v - jnp.mean(v, axis=-1, keepdims=True) - xn * jnp.mean(v * xn, axis=-1, keepdims=True))

    def dx_out(slot):
        return pltpu.make_async_copy(dxbuf.at[slot], dx_ref.at[peer, b], dx_s.at[slot])

    @pl.when(i >= 2)
    def _():
        dx_out(i % 2).wait()
    dxbuf[i % 2] = (g_ref[0, 0].astype(F32) + dv).astype(BF16)
    dx_out(i % 2).start()

    @pl.when(i == SHARDS * BATCH - 1)
    def _():
        copies = [remote(smalls.at[0], smalls.at[o], sm_s.at[o], sm_r.at[o], (0,) + at.peer(o))
                  for o in range(1, SHARDS)]
        for copy in copies:
            copy.start()
        for copy in copies:
            copy.wait()
        total = smalls[at.slot(0)]
        for r in range(1, SHARDS):
            total += smalls[at.slot(r)]
        sum_ref[...] = total
        red.last(LATE - 1)
        for slot in range(SENDS):
            (y_out(slot).wait_send if slot < SENDS - BATCH else y_kept(slot).wait)()
        most = y_ref.at[0:(SHARDS - 1) * BATCH]
        pltpu.make_async_copy(most, most, y_r).wait()
        for slot in range(2):
            dx_out(slot).wait()
        for k in range(LATE):
            red.own_sent(k)
        red.finish(LATE)


def tokens(w, wo, late, grads, small, ln_g, b_out, a, dq, dk, dv, x, g):
    hbm = pl.BlockSpec(memory_space=pl.ANY)
    vec = pl.BlockSpec((1, MODEL), lambda i: (0, 0))
    rows = pl.BlockSpec((8, MODEL), lambda i: (0, 0))
    tile = pl.BlockSpec((1, 1, RUN, MODEL), lambda i: (SHARDS - 1 - i // BATCH, i % BATCH, 0, 0))
    return pl.pallas_call(
        tokens_kernel, grid=(SHARDS * BATCH,),
        in_specs=[hbm, hbm, hbm, hbm, rows, vec, vec] + [tile] * 6,
        out_specs=[hbm, hbm, hbm, rows],
        out_shape=[jax.ShapeDtypeStruct(grads.shape, F32), jax.ShapeDtypeStruct((SHARDS * BATCH, RUN, MODEL), BF16),
                   jax.ShapeDtypeStruct((SHARDS, BATCH, RUN, MODEL), BF16), jax.ShapeDtypeStruct((8, MODEL), F32)],
        scratch_shapes=[
            pltpu.VMEM((3 * MODEL, MODEL), BF16), pltpu.VMEM((MODEL, MODEL), BF16),
            pltpu.VMEM((SENDS, RUN, MODEL), BF16), pltpu.VMEM((2, RUN, MODEL), BF16), pltpu.VMEM((SHARDS, 8, MODEL), F32),
            DMA, DMA, DMA((LATE,)), DMA((SENDS,)), DMA, DMA((2,)), DMA((SHARDS,)), DMA((SHARDS,))] + REDUCE_SCRATCH,
        input_output_aliases={3: 0},
        name="tokens",
        compiler_params=pltpu.CompilerParams(collective_id=1, has_side_effects=True, vmem_limit_bytes=63 << 20),
        cost_estimate=pl.CostEstimate(flops=100_000_000_000, transcendentals=0, bytes_accessed=100 << 20),
    )(w, wo, late, grads, small, ln_g.reshape(1, MODEL), b_out.reshape(1, MODEL), a, dq, dk, dv, x, g)


def copy_kernel(src_ref, dst_ref):
    dst_ref[...] = src_ref[...]


def settle(v):
    blk = pl.BlockSpec((BATCH, RUN, MODEL), lambda i: (i, 0, 0))
    return pl.pallas_call(
        copy_kernel, grid=(SHARDS,), in_specs=[blk], out_specs=blk, out_shape=jax.ShapeDtypeStruct(v.shape, v.dtype),
        name="settle", cost_estimate=pl.CostEstimate(flops=5_000_000_000, transcendentals=0, bytes_accessed=1 << 24),
    )(v)


def solution(mesh):
    mesh4 = Mesh(mesh.devices.reshape(1, 2, 2, 2), ('dp',) + AXES)
    tok = P('dp', AXES, None)
    part = P('dp')

    def local_step(x, g, ln_g, ln_b, w_qkv, b_qkv, w_out, b_out):
        w_rows = jnp.transpose(w_qkv, (1, 2, 3, 0)).reshape(3, PAIRS, LANES, MODEL)
        bias = jnp.transpose(b_qkv.reshape(3, PAIRS // 2, 2, LANES), (1, 0, 2, 3)).reshape(PAIRS // 2, 1, 6 * LANES)
        wo = w_out.reshape(PAIRS, LANES, MODEL)
        grads, xt, gt, late, a, dq, dk, dv, small = head_pairs(x, g, ln_g, ln_b, w_rows, wo, bias)
        grads, y, dx, small = tokens(w_rows.reshape(3 * MODEL, MODEL), wo.reshape(MODEL, MODEL), late, grads, small,
                                     ln_g, b_out, a, dq, dk, dv, xt, gt)
        dx = lax.all_to_all(dx, AXES, 0, 0, tiled=True)
        d_w_qkv = jnp.transpose(grads[:3].reshape(3, HEADS, HEAD, MODEL), (3, 0, 1, 2))
        d_w_out = grads[3].reshape(HEADS, HEAD, MODEL)
        return (settle(y), settle(dx.reshape(x.shape)), small[4], small[5], d_w_qkv, small[:3].reshape(3, HEADS, HEAD), d_w_out,
                small[3])

    return jax.shard_map(local_step, mesh=mesh4, in_specs=(tok, tok) + (P(),) * 6,
                         out_specs=(tok, tok) + (part,) * 6, check_vma=False)
```

profile of v0, /device:TPU:0, one launch (start us, length us, event | category | flops | bytes accessed | tf_op | source)
XLA Modules:
  0.0 968.9 jit_solution(17785448921029393236)
XLA Ops:
  0.6 0.9 reshape.51
  1.5 0.6 copy.17
  2.1 687.3 %head_pairs.1 = (f32[4,16,128,2048]{3,2,1,0:T(8,128)}, bf16[8,2,128,2048]{3,2,1,0:T(8,128)(2,1)}, bf16[8,2,128,2048]{3,2,1,0:T(8,128)(2,1)}, f32[2,4,128,1024]{3...) custom-call(bf16[16,128,2048]{2,1,0:T(8,128)(2,1)} %x_ref.1, ...), custom_call_target="tpu_custom_call" | custom-call | flops 499999997952 | bytes 104857600 | tf_op jit(solution)/shard_map/head_pairs/pallas_call | solution.py:398
  689.4 172.8 %tokens.1 = (f32[4,16,128,2048]{3,2,1,0:T(8,128)}, bf16[16,128,2048]{2,1,0:T(8,128)(2,1)}, bf16[8,2,128,2048]{3,2,1,0:T(8,128)(2,1)}, f32[8,2048]{1,0:T(8,128)}) custom-call(bf16[6144,2048]{1,0:T(8,128)(2,1)} %bitcast.28, bf16[2048,2048]{1,0:T(8,128)(2,1)} %bitcast.30, ...), custom_call_target="tpu_custom_call", output_to_operand_aliasing={{0}: (3, {})} | custom-call | flops 99999997952 | bytes 104857600 | tf_op jit(solution)/shard_map/tokens/pallas_call | solution.py:534
  862.2 3.7 all-to-all-start
  865.9 11.8 %slice.22 = f32[1,16,128,2048]{3,2,1,0:T(8,128)} slice(f32[4,16,128,2048]{3,2,1,0:T(8,128)} %get-tuple-element.33), slice={[3:4], [0:16], [0:128], [0:2048]} | slice | bytes 33554432 | tf_op jit(solution)/shard_map/slice | solution.py:577
  877.8 0.0 copy-start
  877.8 34.5 %slice.20 = f32[3,16,128,2048]{3,2,1,0:T(8,128)} slice(f32[4,16,128,2048]{3,2,1,0:T(8,128)} %get-tuple-element.33), slice={[0:3], [0:16], [0:128], [0:2048]} | slice | bytes 100663296 | tf_op jit(solution)/shard_map/slice | solution.py:576
  912.3 0.0 copy-done
  912.3 0.7 reshape.56
  913.0 0.6 fusion
  913.6 8.9 settle.2
  922.6 37.3 %all-to-all-done = bf16[8,2,128,2048]{3,2,1,0:T(8,128)(2,1)} async-done(((bf16[8,2,128,2048]{3,2,1,0:T(8,128)(2,1)}), bf16[8,2,128,2048]{3,2,1,0:T(8,128)(2,1)}, u32[]{:S(2)}, u32[]{:S(2)}) %all-to-all-start) | async-done | bytes 8388640 | tf_op jit(solution)/shard_map/all_to_all | solution.py:575
  959.9 8.9 settle.3
  (1 shorter events, 0.0 us)
Async XLA Ops:
  862.2 97.7 %all-to-all-start = ((bf16[8,2,128,2048]{3,2,1,0:T(8,128)(2,1)}), bf16[8,2,128,2048]{3,2,1,0:T(8,128)(2,1)}, u32[]{:S(2)}, u32[]{:S(2)}) async-start(bf16[8,2,128,2048]{3,2,1,0:T(8,128)(2,1)} %get-tuple-element.31), calls=%async_computation | async-start | bytes 16777216 | tf_op jit(solution)/shard_map/all_to_all | solution.py:575
  877.8 34.5 %copy-start = (f32[8,2048]{1,0:T(8,128)S(1)}, f32[8,2048]{1,0:T(8,128)}, u32[]{:S(2)}) copy-start(f32[8,2048]{1,0:T(8,128)} %get-tuple-element.32) | copy-start | bytes 196612
where the time goes:
time: 970 us; the launch traced here: 969 us
  Pallas kernels  878 us (91%)
  local copies, waits for them, and re-layouts  49.2 us (5%)
  waiting for transfers between devices  37.3 us (4%)
    pallas_call x1, Pallas kernels, head_pairs(): pl.pallas_call(pairs_kernel, grid=(PAIRS,), in_specs=[hbm, hbm, vec, vec,...  687 us
    pallas_call x1, Pallas kernels, tokens(): pl.pallas_call(tokens_kernel, grid=(SHARDS * BATCH,), in_specs=[hbm, hbm,...  173 us
    all_to_all x1, waiting for transfers between devices, local_step(): dx = lax.all_to_all(dx, AXES, 0, 0, tiled=True)  37.3 us
    slice x1, local copies, waits for them, and re-layouts, local_step(): grads[:3].reshape(3, HEADS, HEAD, MODEL)  34.5 us
  transfers between devices with their start and end apart: 1, of which 1 were waited for; matrix products, arithmetic and copies ran while one was open for 5% of the time, Pallas kernels for 1%

commit v1 on v0

--- a/solution.py
+++ b/solution.py
@@ -15,6 +15,7 @@
 SEQ = SHARDS * RUN
 TOKENS = SEQ * BATCH
 PAIRS = HEADS // 2
+SPLIT = 2
 LATE = 2
 EARLY = PAIRS - LATE
 SENDS = 8
@@ -57,74 +58,76 @@
 
 
 class Reduce:
-    def __init__(self, at, out_ref, base, part, recv1, recv2, sems):
-        self.at, self.out, self.base = at, out_ref, base
+    def __init__(self, at, out_ref, base, split, part, recv1, recv2, sems):
+        self.at, self.out, self.base, self.split = at, out_ref, base, split
         self.part, self.recv1, self.recv2 = part, recv1, recv2
         (self.rs1_s, self.rs1_r, self.rs2_s, self.rs2_r, self.ag_s, self.n1_r, self.n2_r, self.fw_r,
          self.fw_s, self.core_s, self.core_r) = sems
-        self.cols = pl.ds(pl.multiple_of(at.core * HALF, HALF), HALF)
-
-    def piece(self, t, k):
-        return self.out.at[t, self.base + k, :, self.cols]
-
-    def rs1(self, k):
+
+    def cols(self, c):
+        width = HALF // self.split
+        return pl.ds(c * width, width)
+
+    def piece(self, t, c, k):
+        width = HALF // self.split
+        return self.out.at[t, self.base + k, :, pl.ds(pl.multiple_of(self.at.core * HALF + c * width, width), width)]
+
+    def rs1(self, c, k, source=None):
+        s, away = k % 2, pl.ds((1 - self.at.c1) * 2, 2)
+        source = self.part.at[s] if source is None else source
+        return remote(source.at[away, :, self.cols(c)], self.recv1.at[s, :, :, self.cols(c)],
+                      self.rs1_s.at[c, s], self.rs1_r.at[c, s], self.at.n1)
+
+    def rs2(self, c, k):
         s = k % 2
-        return remote(self.part.at[s, pl.ds((1 - self.at.c1) * 2, 2)], self.recv1.at[s],
-                      self.rs1_s.at[s], self.rs1_r.at[s], self.at.n1)
-
-    def rs2(self, k):
-        s = k % 2
-        return remote(self.part.at[s, self.at.c1 * 2 + 1 - self.at.c2], self.recv2.at[s],
-                      self.rs2_s.at[s], self.rs2_r.at[s], self.at.n2)
-
-    def own(self, k):
+        return remote(self.part.at[s, self.at.c1 * 2 + 1 - self.at.c2, :, self.cols(c)],
+                      self.recv2.at[s, :, self.cols(c)], self.rs2_s.at[c, s], self.rs2_r.at[c, s], self.at.n2)
+
+    def own(self, c, k):
         s, t = k % 2, self.at.c1 * 2 + self.at.c2
-        src, dst = self.part.at[s, t], self.piece(t, k)
-        return (remote(src, dst, self.ag_s.at[s, 0], self.n1_r.at[s], self.at.n1),
-                remote(src, dst, self.ag_s.at[s, 1], self.n2_r.at[s], self.at.n2),
-                remote(src, dst, self.ag_s.at[s, 2], self.core_r, self.at.mate),
-                pltpu.make_async_copy(src, dst, self.ag_s.at[s, 3]))
-
-    def to_mate(self, t, k):
-        at = self.piece(t, k)
+        src, dst = self.part.at[s, t, :, self.cols(c)], self.piece(t, c, k)
+        sems = [self.ag_s.at[c, s, n] for n in range(4)]
+        return (remote(src, dst, sems[0], self.n1_r.at[c, s], self.at.n1),
+                remote(src, dst, sems[1], self.n2_r.at[c, s], self.at.n2),
+                remote(src, dst, sems[2], self.core_r, self.at.mate), pltpu.make_async_copy(src, dst, sems[3]))
+
+    def to_mate(self, t, c, k):
+        at = self.piece(t, c, k)
         remote(at, at, self.core_s, self.core_r, self.at.mate).start()
 
-    def arrived(self, t, k, sem):
-        pltpu.make_async_copy(self.piece(t, k), self.piece(t, k), sem).wait()
-
-    def scatter1(self, k):
-        self.rs1(k).start()
-
-    def scatter2(self, k):
-        s, keep = k % 2, pl.ds(self.at.c1 * 2, 2)
-        self.rs1(k).wait()
-        self.part[s, keep] = self.part[s, keep] + self.recv1[s]
-        self.rs2(k).start()
-
-    def gather(self, k):
-        s, t = k % 2, self.at.c1 * 2 + self.at.c2
-        self.rs2(k).wait()
-        self.part[s, t] = self.part[s, t] + self.recv2[s]
-        for copy in self.own(k):
+    def arrived(self, t, c, k, sem):
+        pltpu.make_async_copy(self.piece(t, c, k), self.piece(t, c, k), sem).wait()
+
+    def scatter2(self, c, k, source=None):
+        s, keep, cols = k % 2, pl.ds(self.at.c1 * 2, 2), self.cols(c)
+        self.rs1(c, k, source).wait()
+        self.part[s, keep, :, cols] = self.part[s, keep, :, cols] + self.recv1[s, :, :, cols]
+        self.rs2(c, k).start()
+
+    def gather(self, c, k):
+        s, t, cols = k % 2, self.at.c1 * 2 + self.at.c2, self.cols(c)
+        self.rs2(c, k).wait()
+        self.part[s, t, :, cols] = self.part[s, t, :, cols] + self.recv2[s, :, cols]
+        for copy in self.own(c, k):
             copy.start()
 
-    def forward(self, k):
+    def forward(self, c, k):
         s = k % 2
         t_n2, t_n1 = self.at.c1 * 2 + 1 - self.at.c2, (1 - self.at.c1) * 2 + self.at.c2
-        self.arrived(t_n2, k, self.n2_r.at[s])
-        at = self.piece(t_n2, k)
-        remote(at, at, self.fw_s, self.fw_r.at[s], self.at.n1).start()
-        self.to_mate(t_n2, k)
-        self.arrived(t_n1, k, self.n1_r.at[s])
-        self.to_mate(t_n1, k)
-
-    def last(self, k):
+        self.arrived(t_n2, c, k, self.n2_r.at[c, s])
+        at = self.piece(t_n2, c, k)
+        remote(at, at, self.fw_s, self.fw_r.at[c, s], self.at.n1).start()
+        self.to_mate(t_n2, c, k)
+        self.arrived(t_n1, c, k, self.n1_r.at[c, s])
+        self.to_mate(t_n1, c, k)
+
+    def last(self, c, k):
         t = (1 - self.at.c1) * 2 + 1 - self.at.c2
-        self.arrived(t, k, self.fw_r.at[k % 2])
-        self.to_mate(t, k)
-
-    def own_sent(self, k):
-        *sent, kept = self.own(k)
+        self.arrived(t, c, k, self.fw_r.at[c, k % 2])
+        self.to_mate(t, c, k)
+
+    def own_sent(self, c, k):
+        *sent, kept = self.own(c, k)
         for copy in sent:
             copy.wait_send()
         kept.wait()
@@ -137,9 +140,10 @@
             pltpu.make_async_copy(ref, ref, sem).wait()
 
 
-REDUCE_SCRATCH = [
-    pltpu.VMEM((2, 4, LANES, HALF), F32), pltpu.VMEM((2, 2, LANES, HALF), F32), pltpu.VMEM((2, LANES, HALF), F32),
-    DMA((2,)), DMA((2,)), DMA((2,)), DMA((2,)), DMA((2, 4)), DMA((2,)), DMA((2,)), DMA((2,)), DMA, DMA, DMA]
+def reduce_scratch(split):
+    two = DMA((split, 2))
+    return [pltpu.VMEM((2, 4, LANES, HALF), F32), pltpu.VMEM((2, 2, LANES, HALF), F32),
+            pltpu.VMEM((2, LANES, HALF), F32), two, two, two, two, DMA((split, 2, 4)), two, two, two, DMA, DMA, DMA]
 
 
 def fold(v, op):
@@ -224,13 +228,18 @@
 
 def pairs_kernel(x_ref, g_ref, lg_ref, lb_ref, w_ref, wo_ref, b_ref,
                  out_ref, xt_ref, gt_ref, late_ref, a_ref, dq_ref, dk_ref, dv_ref, small_ref,
-                 h, g, qkv, da, lhs_t, kt, vt, dk_acc, dv_acc, away, met,
-                 x_s, x_r, g_s, g_r, keep_s, late_s, met_s, met_r, part, recv1, recv2, *sems):
+                 h, g, w, wo, qkv, da, lhs_t, kt, vt, dk_acc, dv_acc, away, met,
+                 w_s, wo_s, x_s, x_r, g_s, g_r, keep_s, late_s, met_s, met_r, part, recv1, recv2, *sems):
     j = pl.program_id(0)
     par = j % 2
     at = Place()
-    red = Reduce(at, out_ref, 0, part, recv1, recv2, sems)
+    red = Reduce(at, out_ref, 0, SPLIT, part, recv1, recv2, sems)
     slots = [at.slot(r) for r in range(SHARDS)]
+
+    def weights(q):
+        two, slot = pl.ds(q * 2, 2), q % 2
+        return (pltpu.make_async_copy(w_ref.at[:, two], w.at[slot], w_s.at[slot]),
+                pltpu.make_async_copy(wo_ref.at[two], wo.at[slot], wo_s.at[slot]))
 
     def send_x(u):
         py, px, pc = at.peer(u)
@@ -258,6 +267,8 @@
         for b in range(BATCH):
             for u in order:
                 send_g(b, u).start()
+        for copy in weights(0):
+            copy.start()
         for u in (0, 4, 1, 2, 3, 5, 6, 7):
             pltpu.make_async_copy(h.at[u], h.at[u], x_r.at[u]).wait()
             out = pltpu.make_async_copy(h.at[u], xt_ref.at[u], keep_s)
@@ -269,18 +280,29 @@
                 inv = lax.rsqrt(jnp.mean(cen * cen, axis=-1, keepdims=True) + LN_EPS)
                 h[u, b] = ((cen * inv) * lg_ref[...] + lb_ref[...]).astype(BF16)
 
+    q = j // 2
+
     @pl.when(par == 0)
     def _():
-        w = w_ref[...].reshape(6 * LANES, MODEL)
+        for copy in weights(q):
+            copy.wait()
         step = 4
         for r in range(0, SHARDS, step):
             hr = h[r:r + step].reshape(step * BATCH * RUN, MODEL)
-            res = (lax.dot_general(hr, w, NT, preferred_element_type=F32) + b_ref[0]).astype(BF16)
+            res = lax.dot_general(hr, w[q % 2].reshape(6 * LANES, MODEL), NT, preferred_element_type=F32)
             for t in range(6):
-                qkv[t, r:r + step] = res[:, t * LANES:(t + 1) * LANES].reshape(step, BATCH, RUN, LANES)
+                pair = t % 2
+                bias = jnp.concatenate([b_ref[t // 2, pl.ds(q * 4 + pair * 2 + n, 1)] for n in range(2)], axis=1)
+                col = (res[:, t * LANES:(t + 1) * LANES] + bias).astype(BF16)
+                qkv[t, r:r + step] = col.reshape(step, BATCH, RUN, LANES)
+
+    @pl.when((par == 1) & (j < PAIRS - 1))
+    def _():
+        for copy in weights(q + 1):
+            copy.start()
 
     def project_da(b):
-        res = lax.dot_general(g[:, b].reshape(SEQ, MODEL), wo_ref[...].reshape(2 * LANES, MODEL), NT,
+        res = lax.dot_general(g[:, b].reshape(SEQ, MODEL), wo[q % 2].reshape(2 * LANES, MODEL), NT,
                               preferred_element_type=F32).astype(BF16)
         for t in range(2):
             da[t, :, b] = res[:, t * LANES:(t + 1) * LANES].reshape(SHARDS, RUN, LANES)
@@ -290,10 +312,6 @@
         cols = [gathered(qkv, 2 * t + par) for t in range(3)]
         attend(b, slots, *cols, gathered(da, par), a_ref, dq_ref, dk_ref, dv_ref, kt, vt, dk_acc, dv_acc)
 
-    @pl.when(j >= 2)
-    def _():
-        red.gather(j - 2)
-
     @pl.when(j == 0)
     def _():
         for u in range(SHARDS):
@@ -303,7 +321,17 @@
     def _():
         project_da(0)
 
+    def between(c):
+        @pl.when((j >= 1) & (j <= EARLY))
+        def _():
+            red.scatter2(c, j - 1)
+
+        @pl.when(j >= 2)
+        def _():
+            red.forward(c, j - 2)
+
     one(0)
+    between(0)
 
     @pl.when(j == 0)
     def _():
@@ -316,10 +344,7 @@
         project_da(1)
 
     one(1)
-
-    @pl.when(j >= 2)
-    def _():
-        red.forward(j - 2)
+    between(1)
 
     at_pair = pl.ds(pl.multiple_of(j * LANES, LANES), LANES)
     for t, ref in enumerate((dq_ref, dk_ref, dv_ref, a_ref)):
@@ -341,42 +366,51 @@
         small_ref[3:4] = total
         small_ref[4:8] = jnp.zeros((4, MODEL), F32)
 
-    def weight_grad(dst, start):
-        for t in range(0, HALF, 512):
-            cols = pl.ds(pl.multiple_of(start + t, 512), 512)
-            hc = h[:, :, :, cols].reshape(TOKENS, 512)
-            gc = g[:, :, :, cols].reshape(TOKENS, 512)
-            r = lax.dot_general(lhs_t[0:3 * LANES], hc, NN, preferred_element_type=F32)
-            dst[0:3, :, t:t + 512] = r.reshape(3, LANES, 512)
-            dst[3, :, t:t + 512] = lax.dot_general(lhs_t[3 * LANES:], gc, NN, preferred_element_type=F32)
-
-    def meet(k):
-        return remote(away, met.at[k % 2], met_s, met_r.at[k % 2], at.mate)
-
-    @pl.when(j >= 1)
-    def _():
-        meet(j - 1).wait_send()
-    weight_grad(away, (1 - at.core) * HALF)
-    meet(j).start()
+    def weight_grad(dst, c, side):
+        width = HALF // SPLIT
+        cols = pl.ds(pl.multiple_of(side * HALF + c * width, width), width)
+        hc = h[:, :, :, cols].reshape(TOKENS, width)
+        gc = g[:, :, :, cols].reshape(TOKENS, width)
+        r = lax.dot_general(lhs_t[0:3 * LANES], hc, NN, preferred_element_type=F32)
+        dst[0:3, :, red.cols(c)] = r.reshape(3, LANES, width)
+        dst[3, :, red.cols(c)] = lax.dot_general(lhs_t[3 * LANES:], gc, NN, preferred_element_type=F32)
+
+    def meet(c, k):
+        cols = red.cols(c)
+        return remote(away.at[:, :, cols], met.at[k % 2, :, :, cols], met_s.at[c], met_r.at[c, k % 2], at.mate)
+
+    for c in range(SPLIT):
+        @pl.when(j >= 1)
+        def _():
+            meet(c, j - 1).wait_send()
+        weight_grad(away, c, 1 - at.core)
+        meet(c, j).start()
+        if c == 0:
+            @pl.when((j >= 1) & (j <= EARLY))
+            def _():
+                red.gather(0, j - 1)
+
+    @pl.when(j >= 2)
+    def _():
+        for c in range(SPLIT):
+            red.own_sent(c, j - 2)
+
+    for c in range(SPLIT):
+        @pl.when(j >= 2)
+        def _():
+            red.last(c, j - 2)
+        weight_grad(part.at[par], c, at.core)
+        meet(c, j).wait_recv()
+        cols = red.cols(c)
+        part[par, :, :, cols] = part[par, :, :, cols] + met[par, :, :, cols]
+
+        @pl.when(j < EARLY)
+        def _():
+            red.rs1(c, j).start()
 
     @pl.when((j >= 1) & (j <= EARLY))
     def _():
-        red.scatter2(j - 1)
-
-    @pl.when(j >= 2)
-    def _():
-        red.own_sent(j - 2)
-    weight_grad(part.at[par], at.core * HALF)
-
-    @pl.when(j >= 2)
-    def _():
-        red.last(j - 2)
-    meet(j).wait_recv()
-    part[par] = part[par] + met[par]
-
-    @pl.when(j < EARLY)
-    def _():
-        red.scatter1(j)
+        red.gather(1, j - 1)
 
     @pl.when(j >= EARLY)
     def _():
@@ -384,7 +418,8 @@
 
     @pl.when(j == PAIRS - 1)
     def _():
-        meet(PAIRS - 1).wait_send()
+        for c in range(SPLIT):
+            meet(c, PAIRS - 1).wait_send()
         for k in range(LATE):
             pltpu.make_async_copy(part.at[k], late_ref.at[k], late_s.at[k]).wait()
         red.finish(EARLY)
@@ -397,22 +432,22 @@
     runs = (SHARDS, BATCH, RUN, MODEL)
     return pl.pallas_call(
         pairs_kernel, grid=(PAIRS,),
-        in_specs=[hbm, hbm, vec, vec, pl.BlockSpec((3, 2, LANES, MODEL), lambda j: (0, j // 2, 0, 0)),
-                  pl.BlockSpec((2, LANES, MODEL), lambda j: (j // 2, 0, 0)),
-                  pl.BlockSpec((1, 1, 6 * LANES), lambda j: (j // 2, 0, 0))],
+        in_specs=[hbm, hbm, vec, vec, hbm, hbm, pl.BlockSpec((3, HEADS, HEAD), lambda j: (0, 0, 0))],
         out_specs=[hbm, hbm, hbm, hbm, col, col, col, col, pl.BlockSpec((8, MODEL), lambda j: (0, 0))],
         out_shape=[jax.ShapeDtypeStruct((4, PAIRS, LANES, MODEL), F32), jax.ShapeDtypeStruct(runs, BF16),
                    jax.ShapeDtypeStruct(runs, BF16), jax.ShapeDtypeStruct((LATE, 4, LANES, HALF), F32)]
         + [jax.ShapeDtypeStruct(runs, BF16)] * 4 + [jax.ShapeDtypeStruct((8, MODEL), F32)],
         scratch_shapes=[
             pltpu.VMEM(runs, BF16), pltpu.VMEM(runs, BF16),
+            pltpu.VMEM((2, 3, 2, LANES, MODEL), BF16), pltpu.VMEM((2, 2, LANES, MODEL), BF16),
             pltpu.VMEM((6, SHARDS, BATCH, RUN, LANES), BF16), pltpu.VMEM((2, SHARDS, BATCH, RUN, LANES), BF16),
             pltpu.VMEM((4 * LANES, TOKENS), BF16),
             pltpu.VMEM((LANES, SEQ), BF16), pltpu.VMEM((LANES, SEQ), BF16),
             pltpu.VMEM((SEQ, LANES), F32), pltpu.VMEM((SEQ, LANES), F32),
             pltpu.VMEM((4, LANES, HALF), F32), pltpu.VMEM((2, 4, LANES, HALF), F32),
-            DMA((SHARDS,)), DMA((SHARDS,)), DMA((BATCH, SHARDS)), DMA((BATCH, SHARDS)), DMA, DMA((2,)), DMA, DMA((2,))]
-        + REDUCE_SCRATCH,
+            DMA((2,)), DMA((2,)), DMA((SHARDS,)), DMA((SHARDS,)), DMA((BATCH, SHARDS)), DMA((BATCH, SHARDS)), DMA,
+            DMA((2,)), DMA((SPLIT,)), DMA((SPLIT, 2))]
+        + reduce_scratch(SPLIT),
         name="head_pairs",
         compiler_params=pltpu.CompilerParams(collective_id=0, has_side_effects=True, vmem_limit_bytes=63 << 20),
         cost_estimate=pl.CostEstimate(flops=500_000_000_000, transcendentals=0, bytes_accessed=100 << 20),
@@ -426,7 +461,7 @@
                   w_s, wo_s, late_s, y_s, y_r, dx_s, sm_s, sm_r, part, recv1, recv2, *sems):
     i = pl.program_id(0)
     at = Place()
-    red = Reduce(at, out_ref, EARLY, part, recv1, recv2, sems)
+    red = Reduce(at, out_ref, EARLY, 1, part, recv1, recv2, sems)
     u, b = SHARDS - 1 - i // BATCH, i % BATCH
     py, px, pc = at.peer(u)
     peer = py * 4 + px * 2 + pc
@@ -444,16 +479,20 @@
         get_w.start()
         at.meet_all()
         for k in range(LATE):
+            red.rs1(0, k, late_ref.at[k]).start()
+        for k in range(LATE):
             late(k).wait()
-            red.scatter1(k)
         smalls[0] = small_ref[...]
         get_wo.wait()
 
-    for step, tick, k in ((3, red.scatter2, 0), (4, red.scatter2, 1), (7, red.gather, 0), (9, red.gather, 1),
+    def scatter2(c, k):
+        red.scatter2(c, k, late_ref.at[k])
+
+    for step, tick, k in ((3, scatter2, 0), (4, scatter2, 1), (7, red.gather, 0), (9, red.gather, 1),
                           (10, red.forward, 0), (12, red.forward, 1), (13, red.last, 0)):
         @pl.when(i == step)
         def _(tick=tick, k=k):
-            tick(k)
+            tick(0, k)
 
     s = i % SENDS
     row = at.me * BATCH + b
@@ -514,7 +553,7 @@
         for r in range(1, SHARDS):
             total += smalls[at.slot(r)]
         sum_ref[...] = total
-        red.last(LATE - 1)
+        red.last(0, LATE - 1)
         for slot in range(SENDS):
             (y_out(slot).wait_send if slot < SENDS - BATCH else y_kept(slot).wait)()
         most = y_ref.at[0:(SHARDS - 1) * BATCH]
@@ -522,7 +561,7 @@
         for slot in range(2):
             dx_out(slot).wait()
         for k in range(LATE):
-            red.own_sent(k)
+            red.own_sent(0, k)
         red.finish(LATE)
 
 
@@ -540,7 +579,7 @@
         scratch_shapes=[
             pltpu.VMEM((3 * MODEL, MODEL), BF16), pltpu.VMEM((MODEL, MODEL), BF16),
             pltpu.VMEM((SENDS, RUN, MODEL), BF16), pltpu.VMEM((2, RUN, MODEL), BF16), pltpu.VMEM((SHARDS, 8, MODEL), F32),
-            DMA, DMA, DMA((LATE,)), DMA((SENDS,)), DMA, DMA((2,)), DMA((SHARDS,)), DMA((SHARDS,))] + REDUCE_SCRATCH,
+            DMA, DMA, DMA((LATE,)), DMA((SENDS,)), DMA, DMA((2,)), DMA((SHARDS,)), DMA((SHARDS,))] + reduce_scratch(1),
         input_output_aliases={3: 0},
         name="tokens",
         compiler_params=pltpu.CompilerParams(collective_id=1, has_side_effects=True, vmem_limit_bytes=63 << 20),
@@ -548,15 +587,25 @@
     )(w, wo, late, grads, small, ln_g.reshape(1, MODEL), b_out.reshape(1, MODEL), a, dq, dk, dv, x, g)
 
 
-def copy_kernel(src_ref, dst_ref):
-    dst_ref[...] = src_ref[...]
+def settle_kernel(src_ref, dst_ref, buf, in_s, out_s):
+    rows = lambda ref, i: ref.at[pl.ds(i * BATCH, BATCH)]
+    get = [pltpu.make_async_copy(rows(src_ref, i), rows(buf, i), in_s.at[i]) for i in range(SHARDS)]
+    put = [pltpu.make_async_copy(rows(buf, i), rows(dst_ref, i), out_s.at[i]) for i in range(SHARDS)]
+    for copy in get:
+        copy.start()
+    for i in range(SHARDS):
+        get[i].wait()
+        put[i].start()
+    for copy in put:
+        copy.wait()
 
 
 def settle(v):
-    blk = pl.BlockSpec((BATCH, RUN, MODEL), lambda i: (i, 0, 0))
+    hbm = pl.BlockSpec(memory_space=pl.ANY)
     return pl.pallas_call(
-        copy_kernel, grid=(SHARDS,), in_specs=[blk], out_specs=blk, out_shape=jax.ShapeDtypeStruct(v.shape, v.dtype),
-        name="settle", cost_estimate=pl.CostEstimate(flops=5_000_000_000, transcendentals=0, bytes_accessed=1 << 24),
+        settle_kernel, in_specs=[hbm], out_specs=hbm, out_shape=jax.ShapeDtypeStruct(v.shape, v.dtype),
+        scratch_shapes=[pltpu.VMEM(v.shape, v.dtype), DMA((SHARDS,)), DMA((SHARDS,))], name="settle",
+        cost_estimate=pl.CostEstimate(flops=5_000_000_000, transcendentals=0, bytes_accessed=1 << 24),
     )(v)
 
 
@@ -567,9 +616,8 @@
 
     def local_step(x, g, ln_g, ln_b, w_qkv, b_qkv, w_out, b_out):
         w_rows = jnp.transpose(w_qkv, (1, 2, 3, 0)).reshape(3, PAIRS, LANES, MODEL)
-        bias = jnp.transpose(b_qkv.reshape(3, PAIRS // 2, 2, LANES), (1, 0, 2, 3)).reshape(PAIRS // 2, 1, 6 * LANES)
         wo = w_out.reshape(PAIRS, LANES, MODEL)
-        grads, xt, gt, late, a, dq, dk, dv, small = head_pairs(x, g, ln_g, ln_b, w_rows, wo, bias)
+        grads, xt, gt, late, a, dq, dk, dv, small = head_pairs(x, g, ln_g, ln_b, w_rows, wo, b_qkv)
         grads, y, dx, small = tokens(w_rows.reshape(3 * MODEL, MODEL), wo.reshape(MODEL, MODEL), late, grads, small,
                                      ln_g, b_out, a, dq, dk, dv, xt, gt)
         dx = lax.all_to_all(dx, AXES, 0, 0, tiled=True)

time: 970 us -> 959 us (0.989)
  Pallas kernels: 878 us -> 867 us
where the time goes in v1:
time: 959 us
  Pallas kernels  867 us (90%)
  local copies, waits for them, and re-layouts  47.7 us (5%)
  waiting for transfers between devices  39.9 us (4%)
    pallas_call x1, Pallas kernels, head_pairs(): pl.pallas_call(pairs_kernel, grid=(PAIRS,), in_specs=[hbm, hbm, vec, vec,...  681 us
    pallas_call x1, Pallas kernels, tokens(): pl.pallas_call(tokens_kernel, grid=(SHARDS * BATCH,), in_specs=[hbm, hbm,...  172 us
    all_to_all x1, waiting for transfers between devices, local_step(): dx = lax.all_to_all(dx, AXES, 0, 0, tiled=True)  39.9 us
    slice x1, local copies, waits for them, and re-layouts, local_step(): grads[:3].reshape(3, HEADS, HEAD, MODEL)  34.5 us
  transfers between devices with their start and end apart: 1, of which 1 were waited for; matrix products, arithmetic and copies ran while one was open for 5% of the time, Pallas kernels for 1%

profile of v1, /device:TPU:0, one launch (start us, length us, event | category | flops | bytes accessed | tf_op | source)
XLA Modules:
  0.0 958.6 jit_solution(10973401973492890044)
XLA Ops:
  0.6 681.3 %head_pairs.1 = (f32[4,16,128,2048]{3,2,1,0:T(8,128)}, bf16[8,2,128,2048]{3,2,1,0:T(8,128)(2,1)}, bf16[8,2,128,2048]{3,2,1,0:T(8,128)(2,1)}, f32[2,4,128,1024]{3...) custom-call(bf16[16,128,2048]{2,1,0:T(8,128)(2,1)} %x_ref.1, ...), custom_call_target="tpu_custom_call" | custom-call | flops 499999997952 | bytes 104857600 | tf_op jit(solution)/shard_map/head_pairs/pallas_call | solution.py:433
  682.0 172.4 %tokens.1 = (f32[4,16,128,2048]{3,2,1,0:T(8,128)}, bf16[16,128,2048]{2,1,0:T(8,128)(2,1)}, bf16[8,2,128,2048]{3,2,1,0:T(8,128)(2,1)}, f32[8,2048]{1,0:T(8,128)}) custom-call(bf16[6144,2048]{1,0:T(8,128)(2,1)} %bitcast.24, bf16[2048,2048]{1,0:T(8,128)(2,1)} %bitcast.26, ...), custom_call_target="tpu_custom_call", output_to_operand_aliasing={{0}: (3, {})} | custom-call | flops 99999997952 | bytes 104857600 | tf_op jit(solution)/shard_map/tokens/pallas_call | solution.py:573
  854.4 3.7 all-to-all-start
  858.1 11.8 %slice.22 = f32[1,16,128,2048]{3,2,1,0:T(8,128)} slice(f32[4,16,128,2048]{3,2,1,0:T(8,128)} %get-tuple-element.33), slice={[3:4], [0:16], [0:128], [0:2048]} | slice | bytes 33554432 | tf_op jit(solution)/shard_map/slice | solution.py:625
  869.9 0.0 copy-start
  869.9 34.5 %slice.20 = f32[3,16,128,2048]{3,2,1,0:T(8,128)} slice(f32[4,16,128,2048]{3,2,1,0:T(8,128)} %get-tuple-element.33), slice={[0:3], [0:16], [0:128], [0:2048]} | slice | bytes 100663296 | tf_op jit(solution)/shard_map/slice | solution.py:624
  904.4 0.0 copy-done
  904.4 0.7 reshape.48
  905.1 0.6 fusion
  905.8 6.4 settle.2
  912.2 39.9 %all-to-all-done = bf16[8,2,128,2048]{3,2,1,0:T(8,128)(2,1)} async-done(((bf16[8,2,128,2048]{3,2,1,0:T(8,128)(2,1)}), bf16[8,2,128,2048]{3,2,1,0:T(8,128)(2,1)}, u32[]{:S(2)}, u32[]{:S(2)}) %all-to-all-start) | async-done | bytes 8388640 | tf_op jit(solution)/shard_map/all_to_all | solution.py:623
  952.1 6.4 settle.3
  (1 shorter events, 0.0 us)
Async XLA Ops:
  854.4 97.7 %all-to-all-start = ((bf16[8,2,128,2048]{3,2,1,0:T(8,128)(2,1)}), bf16[8,2,128,2048]{3,2,1,0:T(8,128)(2,1)}, u32[]{:S(2)}, u32[]{:S(2)}) async-start(bf16[8,2,128,2048]{3,2,1,0:T(8,128)(2,1)} %get-tuple-element.31), calls=%async_computation | async-start | bytes 16777216 | tf_op jit(solution)/shard_map/all_to_all | solution.py:623
  869.9 34.5 %copy-start = (f32[8,2048]{1,0:T(8,128)S(1)}, f32[8,2048]{1,0:T(8,128)}, u32[]{:S(2)}) copy-start(f32[8,2048]{1,0:T(8,128)} %get-tuple-element.32) | copy-start | bytes 196612

commit v2 on v1

v2 whole, which is shorter than its diff:
```python
import jax
import jax.numpy as jnp
from jax import lax
from jax.experimental import pallas as pl
from jax.experimental.pallas import tpu as pltpu
from jax.sharding import Mesh, PartitionSpec as P

LN_EPS = 1e-5
LOG2E = 1.4426950408889634
F32, BF16 = jnp.float32, jnp.bfloat16
NN = (((1,), (0,)), ((), ()))
NT = (((1,), (1,)), ((), ()))
RUN, BATCH, MODEL, HEADS, HEAD = 128, 2, 2048, 32, 64
SHARDS = 8
SEQ = SHARDS * RUN
TOKENS = SEQ * BATCH
PAIRS = HEADS // 2
SPLIT = 2
GROUPS = PAIRS // 2
BLOCKS = SHARDS // 2
DIRECT = 48
STEPS_Y = SHARDS
STEPS = PAIRS + STEPS_Y + BLOCKS * GROUPS
LANES = 2 * HEAD
HALF = MODEL // 2
MESH = pl.DeviceIdType.MESH
AXES = ('y', 'x', 'core')
DMA = pltpu.SemaphoreType.DMA


class Place:
    def __init__(self):
        self.y, self.x, self.core = (lax.axis_index(n) for n in AXES)
        y, x, core = self.y, self.x, self.core
        self.me = y * 4 + x * 2 + core
        self.c1 = (1 - core) * x + core * y
        self.c2 = (1 - core) * y + core * x
        self.n1 = (0, y + core * (1 - 2 * y), x + (1 - core) * (1 - 2 * x), core)
        self.n2 = (0, y + (1 - core) * (1 - 2 * y), x + core * (1 - 2 * x), core)
        self.mate = (0, y, x, 1 - core)

    def peer(self, u):
        fc, fy, fx = u // 4, (u // 2) % 2, u % 2
        flip = lambda v, f: v + f * (1 - 2 * v)
        return flip(self.y, fy), flip(self.x, fx), flip(self.core, fc)

    def slot(self, run):
        flip = lambda v, f: v + f * (1 - 2 * v)
        return flip(self.core, run % 2) * 4 + flip(self.y, run // 4) * 2 + flip(self.x, (run // 2) % 2)

    def meet_all(self):
        barrier = pltpu.get_barrier_semaphore()
        for u in range(1, SHARDS):
            pl.semaphore_signal(barrier, inc=1, device_id=(0,) + self.peer(u), device_id_type=MESH)
        pl.semaphore_wait(barrier, SHARDS - 1)


def remote(src, dst, send, recv, to):
    return pltpu.make_async_remote_copy(src, dst, send, recv, device_id=to, device_id_type=MESH)


def drain(ref, sem):
    pltpu.make_async_copy(ref, ref, sem).wait()


class Reduce:
    def __init__(self, at, out_ref, split, part, recv1, recv2, sems):
        self.at, self.out, self.split = at, out_ref, split
        self.part, self.recv1, self.recv2 = part, recv1, recv2
        (self.rs1_s, self.rs1_r, self.rs2_s, self.rs2_r, self.ag_s, self.n1_r, self.n2_r, self.fw_r,
         self.fw_s, self.core_s, self.core_r) = sems

    def cols(self, c):
        width = HALF // self.split
        return pl.ds(c * width, width)

    def piece(self, t, c, k):
        width = HALF // self.split
        return self.out.at[t, k, :, pl.ds(pl.multiple_of(self.at.core * HALF + c * width, width), width)]

    def rs1(self, c, k):
        s, away = k % 2, pl.ds((1 - self.at.c1) * 2, 2)
        return remote(self.part.at[s, away, :, self.cols(c)], self.recv1.at[s, :, :, self.cols(c)],
                      self.rs1_s.at[c, s], self.rs1_r.at[c, s], self.at.n1)

    def rs2(self, c, k):
        s = k % 2
        return remote(self.part.at[s, self.at.c1 * 2 + 1 - self.at.c2, :, self.cols(c)],
                      self.recv2.at[s, :, self.cols(c)], self.rs2_s.at[c, s], self.rs2_r.at[c, s], self.at.n2)

    def own(self, c, k):
        s, t = k % 2, self.at.c1 * 2 + self.at.c2
        src, dst = self.part.at[s, t, :, self.cols(c)], self.piece(t, c, k)
        sems = [self.ag_s.at[c, s, n] for n in range(4)]
        return (remote(src, dst, sems[0], self.n1_r.at[c, s], self.at.n1),
                remote(src, dst, sems[1], self.n2_r.at[c, s], self.at.n2),
                remote(src, dst, sems[2], self.core_r, self.at.mate), pltpu.make_async_copy(src, dst, sems[3]))

    def to_mate(self, t, c, k):
        at = self.piece(t, c, k)
        remote(at, at, self.core_s, self.core_r, self.at.mate).start()

    def arrived(self, t, c, k, sem):
        drain(self.piece(t, c, k), sem)

    def scatter2(self, c, k):
        s, keep, cols = k % 2, pl.ds(self.at.c1 * 2, 2), self.cols(c)
        self.rs1(c, k).wait()
        self.part[s, keep, :, cols] = self.part[s, keep, :, cols] + self.recv1[s, :, :, cols]
        self.rs2(c, k).start()

    def gather(self, c, k):
        s, t, cols = k % 2, self.at.c1 * 2 + self.at.c2, self.cols(c)
        self.rs2(c, k).wait()
        self.part[s, t, :, cols] = self.part[s, t, :, cols] + self.recv2[s, :, cols]
        for copy in self.own(c, k):
            copy.start()

    def forward(self, c, k):
        s = k % 2
        t_n2, t_n1 = self.at.c1 * 2 + 1 - self.at.c2, (1 - self.at.c1) * 2 + self.at.c2
        self.arrived(t_n2, c, k, self.n2_r.at[c, s])
        at = self.piece(t_n2, c, k)
        remote(at, at, self.fw_s, self.fw_r.at[c, s], self.at.n1).start()
        self.to_mate(t_n2, c, k)
        self.arrived(t_n1, c, k, self.n1_r.at[c, s])
        self.to_mate(t_n1, c, k)

    def last(self, c, k):
        t = (1 - self.at.c1) * 2 + 1 - self.at.c2
        self.arrived(t, c, k, self.fw_r.at[c, k % 2])
        self.to_mate(t, c, k)

    def own_sent(self, c, k):
        *sent, kept = self.own(c, k)
        for copy in sent:
            copy.wait_send()
        kept.wait()

    def finish(self):
        half = pl.ds(0, HALF)
        for ref, sem in ((self.out.at[:, :, :, half], self.core_r), (self.out.at[0:3, :, :, half], self.core_s),
                         (self.out.at[0, :, :, half], self.fw_s)):
            drain(ref, sem)


def reduce_scratch(split):
    two = DMA((split, 2))
    return [pltpu.VMEM((2, 4, LANES, HALF), F32), pltpu.VMEM((2, 2, LANES, HALF), F32),
            pltpu.VMEM((2, LANES, HALF), F32), two, two, two, two, DMA((split, 2, 4)), two, two, two, DMA, DMA, DMA]


def fold(v, op):
    r = v[0:8]
    for t in range(8, v.shape[0], 8):
        r = op(r, v[t:t + 8])
    return r


def attend(b, slots, q, k, v, da, a_ref, dq_ref, dk_ref, dv_ref, kt, vt, dk_acc, dv_acc):
    first = lax.broadcasted_iota(jnp.int32, (SEQ, LANES), 1) < HEAD
    zero = jnp.zeros_like(q)
    qm = (jnp.where(first, q, zero), jnp.where(first, zero, q))
    dm = (jnp.where(first, da, zero), jnp.where(first, zero, da))
    kt[...] = k.T
    vt[...] = v.T
    blk, ch = 256, 128
    scale = HEAD ** -0.5
    cc = scale * LOG2E
    dot = lambda l, r, dims=NN: lax.dot_general(l, r, dims, preferred_element_type=F32)

    def scores(i):
        ext, qs = (i + 1) * blk, slice(i * blk, (i + 1) * blk)
        return [(dot(k[:ext], qm[h][qs], NT), dot(v[:ext], dm[h][qs], NT)) for h in range(2)]

    def softmax(i, pair):
        ext = (i + 1) * blk
        s, dp = ([m[t:t + ch] for t in range(0, ext, ch)] for m in pair)
        top = total = cross = None
        for n, t in enumerate(range(0, ext, ch)):
            if t >= i * blk:
                rows = lax.broadcasted_iota(jnp.int32, (ch, blk), 0) + (t - i * blk)
                s[n] = jnp.where(rows <= lax.broadcasted_iota(jnp.int32, (ch, blk), 1), s[n], -jnp.inf)
            f = fold(s[n], jnp.maximum)
            top = f if top is None else jnp.maximum(top, f)
        top = jnp.max(top, axis=0, keepdims=True) * cc
        for n in range(len(s)):
            s[n] = jnp.exp2(s[n] * cc - top)
            f, fx = fold(s[n], jnp.add), fold(s[n] * dp[n], jnp.add)
            total = f if total is None else total + f
            cross = fx if cross is None else cross + fx
        inv = 1.0 / jnp.sum(total, axis=0, keepdims=True)
        c = jnp.sum(cross, axis=0, keepdims=True) * inv
        pb, ds = [], []
        for n in range(len(s)):
            p = s[n] * inv
            pb.append(p.astype(BF16))
            ds.append((p * (dp[n] - c)).astype(BF16))
        return jnp.concatenate(pb, axis=0), jnp.concatenate(ds, axis=0)

    def outputs(i, pd):
        old, ext = i * blk, (i + 1) * blk
        qs = slice(old, ext)
        both = lambda m: jnp.concatenate([m[0][qs], m[1][qs]], axis=0)
        halves = [slice(0, HEAD), slice(HEAD, LANES)]
        o = jnp.concatenate([dot(vt[halves[h], :ext], pd[h][0]) for h in range(2)], axis=0)
        dq = jnp.concatenate([dot(kt[halves[h], :ext], pd[h][1]) for h in range(2)], axis=0)
        dv = dot(jnp.concatenate([pd[0][0], pd[1][0]], axis=1), both(dm))
        dk = dot(jnp.concatenate([pd[0][1], pd[1][1]], axis=1), both(qm))
        if old:
            dv_acc[:old] += dv[:old]
            dk_acc[:old] += dk[:old]
        dv_acc[old:ext] = dv[old:]
        dk_acc[old:ext] = dk[old:]
        o, dq = o.T.astype(BF16), (dq.T * scale).astype(BF16)
        for r in range(2):
            a_ref[slots[2 * i + r], b] = o[r * RUN:(r + 1) * RUN]
            dq_ref[slots[2 * i + r], b] = dq[r * RUN:(r + 1) * RUN]

    count = SEQ // blk
    ready = scores(0)
    for i in range(count):
        pd = [softmax(i, ready[h]) for h in range(2)]
        if i + 1 < count:
            ready = scores(i + 1)
        outputs(i, pd)
    for r in range(SHARDS):
        run = slice(r * RUN, (r + 1) * RUN)
        dk_ref[slots[r], b] = (dk_acc[run] * scale).astype(BF16)
        dv_ref[slots[r], b] = dv_acc[run].astype(BF16)


def pair_step(j, at, red, x_ref, g_ref, lg_ref, lb_ref, w_ref, wo_ref, b_ref, xt_ref, gt_ref, d_ref,
              h, g, w, wo, qkv, da, lhs_t, kt, vt, dk_acc, dv_acc, away, met, made, smalls,
              w_s, wo_s, x_s, x_r, g_s, g_r, keep_s, met_s, met_r, made_s):
    par = j % 2
    part = red.part
    slots = [at.slot(r) for r in range(SHARDS)]
    dq_ref, dk_ref, dv_ref, a_ref = (made.at[par, t] for t in range(4))

    def weights(q):
        two, slot = pl.ds(q * 2, 2), q % 2
        return (pltpu.make_async_copy(w_ref.at[:, two], w.at[slot], w_s.at[slot]),
                pltpu.make_async_copy(wo_ref.at[q], wo.at[slot], wo_s.at[slot]))

    def send_x(u):
        py, px, pc = at.peer(u)
        rows = x_ref.at[pl.ds((py * 4 + px * 2 + pc) * BATCH, BATCH)]
        if u == 0:
            return pltpu.make_async_copy(rows, h.at[0], x_r.at[0])
        return remote(rows, h.at[u], x_s.at[u], x_r.at[u], (0, py, px, pc))

    def send_g(b, u):
        py, px, pc = at.peer(u)
        row = g_ref.at[(py * 4 + px * 2 + pc) * BATCH + b]
        if u == 0:
            return pltpu.make_async_copy(row, g.at[0, b], g_r.at[b, 0])
        return remote(row, g.at[u, b], g_s.at[b, u], g_r.at[b, u], (0, py, px, pc))

    def g_landed(b, u):
        drain(g.at[u, b], g_r.at[b, u])

    @pl.when(j == 0)
    def _():
        at.meet_all()
        order = (0, 3, 1, 2, 7, 5, 6, 4)
        for u in order:
            send_x(u).start()
        for b in range(BATCH):
            for u in order:
                send_g(b, u).start()
        for copy in weights(0):
            copy.start()

        @pl.loop(0, SHARDS)
        def _(u):
            drain(h.at[u], x_r.at[u])
            out = pltpu.make_async_copy(h.at[u], xt_ref.at[u], keep_s)
            out.start()
            out.wait()
            for b in range(BATCH):
                xf = h[u, b].astype(F32)
                cen = xf - jnp.mean(xf, axis=-1, keepdims=True)
                inv = lax.rsqrt(jnp.mean(cen * cen, axis=-1, keepdims=True) + LN_EPS)
                h[u, b] = ((cen * inv) * lg_ref[...] + lb_ref[...]).astype(BF16)

    q = j // 2

    @pl.when(par == 0)
    def _():
        for copy in weights(q):
            copy.wait()
        step = 4
        for r in range(0, SHARDS, step):
            hr = h[r:r + step].reshape(step * BATCH * RUN, MODEL)
            res = lax.dot_general(hr, w[q % 2].reshape(6 * LANES, MODEL), NT, preferred_element_type=F32)
            for t in range(6):
                pair = t % 2
                bias = jnp.concatenate([b_ref[t // 2, pl.ds(q * 4 + pair * 2 + n, 1)] for n in range(2)], axis=1)
                col = (res[:, t * LANES:(t + 1) * LANES] + bias).astype(BF16)
                qkv[t, r:r + step] = col.reshape(step, BATCH, RUN, LANES)

    @pl.when((par == 1) & (j < PAIRS - 1))
    def _():
        for copy in weights(q + 1):
            copy.start()

    def project_da(b):
        res = lax.dot_general(g[:, b].reshape(SEQ, MODEL), wo[q % 2].reshape(2 * LANES, MODEL), NT,
                              preferred_element_type=F32).astype(BF16)
        for t in range(2):
            da[t, :, b] = res[:, t * LANES:(t + 1) * LANES].reshape(SHARDS, RUN, LANES)

    def one(b):
        gathered = lambda ref, t: jnp.concatenate([ref[t, slots[r], b] for r in range(SHARDS)], axis=0)
        cols = [gathered(qkv, 2 * t + par) for t in range(3)]
        attend(b, slots, *cols, gathered(da, par), a_ref, dq_ref, dk_ref, dv_ref, kt, vt, dk_acc, dv_acc)

    @pl.when(j == 0)
    def _():
        for u in range(SHARDS):
            g_landed(0, u)

    @pl.when(par == 0)
    def _():
        project_da(0)

    def between(c):
        @pl.when(j >= 1)
        def _():
            red.scatter2(c, j - 1)

        @pl.when(j >= 2)
        def _():
            red.forward(c, j - 2)

    @pl.when(j >= 2)
    def _():
        drain(made.at[par], made_s.at[par])

    one(0)
    between(0)

    @pl.when(j == 0)
    def _():
        for u in range(SHARDS):
            g_landed(1, u)
        pltpu.make_async_copy(g, gt_ref, keep_s).start()

    @pl.when(par == 0)
    def _():
        project_da(1)

    one(1)
    between(1)

    at_pair = pl.ds(pl.multiple_of(j * LANES, LANES), LANES)
    pltpu.make_async_copy(made.at[par], d_ref.at[:, :, :, :, at_pair], made_s.at[par]).start()
    for t, ref in enumerate((dq_ref, dk_ref, dv_ref, a_ref)):
        d = ref[...].reshape(TOKENS, LANES)
        lhs_t[t // 2, t % 2] = d.T
        if t < 3:
            smalls[0, t:t + 1, at_pair] = jnp.sum(d.astype(F32), axis=0, keepdims=True)

    @pl.when(j == 1)
    def _():
        for u in range(1, SHARDS):
            send_x(u).wait_send()
            for b in range(BATCH):
                send_g(b, u).wait_send()
        pltpu.make_async_copy(g, gt_ref, keep_s).wait()
        smalls[0, 3:4] = jnp.zeros((1, MODEL), F32)

        @pl.loop(0, SHARDS)
        def _(u):
            smalls[0, 3:4] += jnp.sum(g[u].reshape(BATCH * RUN, MODEL).astype(F32), axis=0, keepdims=True)
        smalls[0, 4:8] = jnp.zeros((4, MODEL), F32)

    def weight_grad(dst, c, side):
        width = HALF // SPLIT
        cols = pl.ds(pl.multiple_of(side * HALF + c * width, width), width)
        hc = h[:, :, :, cols].reshape(TOKENS, width)
        gc = g[:, :, :, cols].reshape(TOKENS, width)
        lhs = lhs_t[...].reshape(4 * LANES, TOKENS)
        r = lax.dot_general(lhs[0:3 * LANES], hc, NN, preferred_element_type=F32)
        dst[0:3, :, red.cols(c)] = r.reshape(3, LANES, width)
        dst[3, :, red.cols(c)] = lax.dot_general(lhs[3 * LANES:], gc, NN, preferred_element_type=F32)

    def meet(c, k):
        return pair_meet(red, at, away, met, met_s, met_r, c, k)

    for c in range(SPLIT):
        @pl.when(j >= 1)
        def _():
            meet(c, j - 1).wait_send()
        weight_grad(away, c, 1 - at.core)
        meet(c, j).start()
        if c == 0:
            @pl.when(j >= 1)
            def _():
                red.gather(0, j - 1)

    @pl.when(j >= 2)
    def _():
        for c in range(SPLIT):
            red.own_sent(c, j - 2)

    for c in range(SPLIT):
        @pl.when(j >= 2)
        def _():
            red.last(c, j - 2)
        weight_grad(part.at[par], c, at.core)
        meet(c, j).wait_recv()
        cols = red.cols(c)
        part[par, :, :, cols] = part[par, :, :, cols] + met[par, :, :, cols]
        red.rs1(c, j).start()

    @pl.when(j >= 1)
    def _():
        red.gather(1, j - 1)


def block_kernel(x_ref, g_ref, lg_ref, lb_ref, w_ref, wo_ref, b_ref, bo_ref,
                 out_ref, y_ref, dxr_ref, dxl_ref, sum_ref, xt_ref, gt_ref, d_ref,
                 h, g, w, wo, qkv, da, lhs_t, kt, vt, dk_acc, dv_acc, away, met, made, smalls,
                 w_s, wo_s, x_s, x_r, g_s, g_r, keep_s, met_s, met_r, made_s, a_s, xb_s, big_s, tile_s, lt_s,
                 y_s, y_r, yk_s, dx_s, dx_r, dxk_s, dxl_s, sm_s, sm_r, part, recv1, recv2, *sems):
    j = pl.program_id(0)
    at = Place()
    red = Reduce(at, out_ref, SPLIT, part, recv1, recv2, sems)

    @pl.when(j < PAIRS)
    def _():
        pair_step(j, at, red, x_ref, g_ref, lg_ref, lb_ref, w_ref, wo_ref, b_ref, xt_ref, gt_ref, d_ref,
                  h, g, w, wo, qkv, da, lhs_t, kt, vt, dk_acc, dv_acc, away, met, made, smalls,
                  w_s, wo_s, x_s, x_r, g_s, g_r, keep_s, met_s, met_r, made_s)

    n = j - PAIRS
    k0, k1 = PAIRS - 2, PAIRS - 1
    for step, ticks in ((3, ((red.scatter2, 0, k1), (red.forward, 0, k0))),
                        (5, ((red.scatter2, 1, k1), (red.forward, 1, k0))),
                        (8, ((red.gather, 0, k1),)),
                        (9, ((red.own_sent, 0, k0), (red.own_sent, 1, k0), (red.last, 0, k0), (red.last, 1, k0))),
                        (11, ((red.gather, 1, k1),)),
                        (18, ((red.forward, 0, k1),)), (22, ((red.forward, 1, k1),)),
                        (32, ((red.last, 0, k1),)), (36, ((red.last, 1, k1),))):
        @pl.when(n == step)
        def _(ticks=ticks):
            for tick, c, k in ticks:
                tick(c, k)

    xbuf = wo

    def a_tile(u):
        return pltpu.make_async_copy(d_ref.at[3, u], lhs_t.at[u % 2], a_s.at[u % 2])

    def x_tile(u):
        return pltpu.make_async_copy(xt_ref.at[u], xbuf.at[u % 2], xb_s.at[u % 2])

    @pl.when(n == 0)
    def _():
        big = pltpu.make_async_copy(wo_ref, g, big_s)
        big.start()
        for u in (7, 6):
            x_tile(u).start()
        for k in (k0, k1):
            drain(made.at[k % 2], made_s.at[k % 2])
        for c in range(SPLIT):
            pair_meet(red, at, away, met, met_s, met_r, c, k1).wait_send()
        for u in (7, 6):
            a_tile(u).start()
        big.wait()

    @pl.when((n >= 0) & (n < STEPS_Y))
    def _():
        u = SHARDS - 1 - n
        py, px, pc = at.peer(u)
        a_tile(u).wait()
        x_tile(u).wait()
        r = jnp.dot(lhs_t[u % 2].reshape(BATCH * RUN, MODEL), g[...].reshape(MODEL, MODEL),
                    preferred_element_type=F32)
        r = xbuf[u % 2].reshape(BATCH * RUN, MODEL).astype(F32) + r + bo_ref[...]
        h[u] = r.astype(BF16).reshape(BATCH, RUN, MODEL)
        rows = y_ref.at[pl.ds(at.me * BATCH, BATCH)]

        @pl.when(u > 0)
        def _():
            remote(h.at[u], rows, y_s, y_r, (0, py, px, pc)).start()

        @pl.when(u == 0)
        def _():
            pltpu.make_async_copy(h.at[u], rows, yk_s).start()

        @pl.when(u >= 2)
        def _():
            a_tile(u - 2).start()
            x_tile(u - 2).start()

    i = n - STEPS_Y

    def d_tiles(i):
        base, q, r = SHARDS - 2 - 2 * (i // GROUPS), i % GROUPS, i % 4
        copies = []
        for t in range(3):
            for p in range(2):
                cols = pl.ds(pl.multiple_of((2 * q + p) * LANES, LANES), LANES)
                copies.append(pltpu.make_async_copy(d_ref.at[t, pl.ds(base, 2), :, :, cols],
                                                    qkv.at[2 * t + p, pl.ds(2 * r, 2)], tile_s.at[r]))
        return copies

    def w_tile(i):
        return pltpu.make_async_copy(w_ref.at[:, pl.ds(i % GROUPS * 2, 2)], w.at[i % 2], w_s.at[i % 2])

    @pl.when(n == STEPS_Y - 1)
    def _():
        w_tile(0).start()
        for ahead in range(2):
            for copy in d_tiles(ahead):
                copy.start()

    @pl.when(i >= 0)
    def _():
        r, q = i % 4, i % GROUPS
        base = SHARDS - 2 - 2 * (i // GROUPS)

        @pl.when(i + 2 < BLOCKS * GROUPS)
        def _():
            for copy in d_tiles(i + 2):
                copy.start()
        w_tile(i).wait()
        drain(qkv.at[:, pl.ds(2 * r, 2)], tile_s.at[r])

        @pl.when(i + 1 < BLOCKS * GROUPS)
        def _():
            w_tile(i + 1).start()
        lhs = jnp.concatenate([qkv[t, pl.ds(2 * r, 2)].reshape(4 * RUN, LANES) for t in range(6)], axis=1)
        res = jnp.dot(lhs, w[i % 2].reshape(6 * LANES, MODEL), preferred_element_type=F32)
        halves = [res[:, s * HALF:(s + 1) * HALF].reshape(4, RUN, HALF) for s in range(2)]

        @pl.when(q == 0)
        def _():
            for s in range(2):
                met[s] = halves[s]

        @pl.when(q > 0)
        def _():
            for s in range(2):
                met[s] = met[s] + halves[s]

        tiles = ((xt_ref, xbuf, xb_s), (gt_ref, lhs_t, lt_s))

        @pl.when(q == GROUPS - 3)
        def _():
            for src, dst, sem in tiles:
                for s in range(2):
                    pltpu.make_async_copy(src.at[base + s], dst.at[s], sem.at[s]).start()

        @pl.when(q == GROUPS - 1)
        def _():
            for src, dst, sem in tiles:
                for s in range(2):
                    pltpu.make_async_copy(src.at[base + s], dst.at[s], sem.at[s]).wait()
            for s in range(2):
                u = base + s
                py, px, pc = at.peer(u)
                for b in range(BATCH):
                    dh = jnp.concatenate([met[0, 2 * s + b], met[1, 2 * s + b]], axis=1)
                    xf = xbuf[s, b].astype(F32)
                    cen = xf - jnp.mean(xf, axis=-1, keepdims=True)
                    inv = lax.rsqrt(jnp.mean(cen * cen, axis=-1, keepdims=True) + LN_EPS)
                    xn = cen * inv
                    smalls[0, 4:5] += jnp.sum(dh * xn, axis=0, keepdims=True)
                    smalls[0, 5:6] += jnp.sum(dh, axis=0, keepdims=True)
                    v = dh * lg_ref[...]
                    v = v - jnp.mean(v, axis=-1, keepdims=True) - xn * jnp.mean(v * xn, axis=-1, keepdims=True)
                    g[u, b] = (lhs_t[s, b].astype(F32) + inv * v).astype(BF16)
                rest = pl.ds(DIRECT, RUN - DIRECT)
                pltpu.make_async_copy(g.at[u, :, rest], dxl_ref.at[py * 4 + px * 2 + pc], dxl_s).start()
                src, dst = g.at[u, :, 0:DIRECT], dxr_ref.at[pl.ds(at.me * BATCH, BATCH)]

                @pl.when(u > 0)
                def _():
                    remote(src, dst, dx_s, dx_r, (0, py, px, pc)).start()

                @pl.when(u == 0)
                def _():
                    pltpu.make_async_copy(src, dst, dxk_s).start()

    @pl.when(j == STEPS - 1)
    def _():
        copies = [remote(smalls.at[0], smalls.at[o], sm_s.at[o], sm_r.at[o], (0,) + at.peer(o))
                  for o in range(1, SHARDS)]
        for copy in copies:
            copy.start()
        for copy in copies:
            copy.wait()
        total = smalls[at.slot(0)]
        for r in range(1, SHARDS):
            total += smalls[at.slot(r)]
        sum_ref[...] = total
        for c in range(SPLIT):
            red.own_sent(c, k1)
        red.finish()
        others = (SHARDS - 1) * BATCH
        drain(h.at[1:SHARDS], y_s)
        drain(y_ref.at[0:others], y_r)
        drain(h.at[0], yk_s)
        drain(g.at[1:SHARDS, :, 0:DIRECT], dx_s)
        drain(dxr_ref.at[0:others], dx_r)
        drain(g.at[0, :, 0:DIRECT], dxk_s)
        drain(dxl_ref, dxl_s)


def pair_meet(red, at, away, met, met_s, met_r, c, k):
    cols = red.cols(c)
    return remote(away.at[:, :, cols], met.at[k % 2, :, :, cols], met_s.at[c], met_r.at[c, k % 2], at.mate)


def block(x, g, ln_g, ln_b, w_rows, wo_rows, bias, b_out):
    hbm = pl.BlockSpec(memory_space=pl.ANY)
    vec = pl.BlockSpec((1, MODEL), lambda j: (0, 0))
    runs = (SHARDS, BATCH, RUN, MODEL)
    heads = (SHARDS, BATCH, RUN, LANES)
    two = DMA((2,))
    return pl.pallas_call(
        block_kernel, grid=(STEPS,),
        in_specs=[hbm, hbm, vec, vec, hbm, hbm, pl.BlockSpec((3, HEADS, HEAD), lambda j: (0, 0, 0)), vec],
        out_specs=[hbm, hbm, hbm, hbm, pl.BlockSpec((8, MODEL), lambda j: (0, 0)), hbm, hbm, hbm],
        out_shape=[jax.ShapeDtypeStruct((4, PAIRS, LANES, MODEL), F32),
                   jax.ShapeDtypeStruct((SHARDS * BATCH, RUN, MODEL), BF16),
                   jax.ShapeDtypeStruct((SHARDS * BATCH, DIRECT, MODEL), BF16),
                   jax.ShapeDtypeStruct((SHARDS, BATCH, RUN - DIRECT, MODEL), BF16),
                   jax.ShapeDtypeStruct((8, MODEL), F32), jax.ShapeDtypeStruct(runs, BF16),
                   jax.ShapeDtypeStruct(runs, BF16), jax.ShapeDtypeStruct((4,) + runs, BF16)],
        scratch_shapes=[
            pltpu.VMEM(runs, BF16), pltpu.VMEM(runs, BF16),
            pltpu.VMEM((2, 3, 2, LANES, MODEL), BF16), pltpu.VMEM((2, 2, LANES, MODEL), BF16),
            pltpu.VMEM((6,) + heads, BF16), pltpu.VMEM((2,) + heads, BF16),
            pltpu.VMEM((2, 2, LANES, TOKENS), BF16),
            pltpu.VMEM((LANES, SEQ), BF16), pltpu.VMEM((LANES, SEQ), BF16),
            pltpu.VMEM((SEQ, LANES), F32), pltpu.VMEM((SEQ, LANES), F32),
            pltpu.VMEM((4, LANES, HALF), F32), pltpu.VMEM((2, 4, LANES, HALF), F32),
            pltpu.VMEM((2, 4) + heads, BF16),
            pltpu.VMEM((SHARDS, 8, MODEL), F32),
            two, two, DMA((SHARDS,)), DMA((SHARDS,)), DMA((BATCH, SHARDS)), DMA((BATCH, SHARDS)), DMA,
            DMA((SPLIT,)), DMA((SPLIT, 2)), two, two, two, DMA, DMA((4,)), two,
            DMA, DMA, DMA, DMA, DMA, DMA, DMA, DMA((SHARDS,)), DMA((SHARDS,))]
        + reduce_scratch(SPLIT),
        name="block",
        compiler_params=pltpu.CompilerParams(collective_id=0, has_side_effects=True, vmem_limit_bytes=67043328),
        cost_estimate=pl.CostEstimate(flops=600_000_000_000, transcendentals=0, bytes_accessed=200 << 20),
    )(x, g, ln_g.reshape(1, MODEL), ln_b.reshape(1, MODEL), w_rows, wo_rows, bias, b_out.reshape(1, MODEL))


def settle_kernel(src_ref, *refs):
    *_, dst_ref, buf, in_s, out_s = refs
    first = dst_ref.shape[1] - src_ref.shape[1] if len(refs) == 5 else 0
    at = pl.ds(first, src_ref.shape[1])
    rows = lambda i: pl.ds(i * BATCH, BATCH)
    get = [pltpu.make_async_copy(src_ref.at[rows(i)], buf.at[rows(i)], in_s.at[i]) for i in range(SHARDS)]
    put = [pltpu.make_async_copy(buf.at[rows(i)], dst_ref.at[rows(i), at], out_s.at[i]) for i in range(SHARDS)]
    for copy in get:
        copy.start()
    for i in range(SHARDS):
        get[i].wait()
        put[i].start()
    for copy in put:
        copy.wait()


def settle(src, onto=None, rows=RUN):
    hbm = pl.BlockSpec(memory_space=pl.ANY)
    size = src.shape[0] * src.shape[1] * src.shape[2] * 4
    return pl.pallas_call(
        settle_kernel, in_specs=[hbm] * (1 if onto is None else 2), out_specs=hbm,
        out_shape=jax.ShapeDtypeStruct((src.shape[0], rows, src.shape[2]), src.dtype),
        scratch_shapes=[pltpu.VMEM(src.shape, src.dtype), DMA((SHARDS,)), DMA((SHARDS,))],
        input_output_aliases={} if onto is None else {1: 0}, name="settle",
        cost_estimate=pl.CostEstimate(flops=5_000_000_000, transcendentals=0, bytes_accessed=size),
    )(*([src] if onto is None else [src, onto]))


def solution(mesh):
    mesh4 = Mesh(mesh.devices.reshape(1, 2, 2, 2), ('dp',) + AXES)
    tok = P('dp', AXES, None)
    part = P('dp')

    def local_step(x, g, ln_g, ln_b, w_qkv, b_qkv, w_out, b_out):
        w_rows = jnp.transpose(w_qkv, (1, 2, 3, 0)).reshape(3, PAIRS, LANES, MODEL)
        wo = w_out.reshape(GROUPS, 2, LANES, MODEL)
        grads, y, dx_head, dx_rest, small, *_ = block(x, g, ln_g, ln_b, w_rows, wo, b_qkv, b_out)
        dx_rest = lax.all_to_all(dx_rest, AXES, 0, 0, tiled=True).reshape(SHARDS * BATCH, RUN - DIRECT, MODEL)
        dx = settle(dx_rest, settle(dx_head))
        d_w_qkv = jnp.transpose(grads[:3].reshape(3, HEADS, HEAD, MODEL), (3, 0, 1, 2))
        d_w_out = grads[3].reshape(HEADS, HEAD, MODEL)
        return (settle(y), dx, small[4], small[5], d_w_qkv, small[:3].reshape(3, HEADS, HEAD), d_w_out, small[3])

    return jax.shard_map(local_step, mesh=mesh4, in_specs=(tok, tok) + (P(),) * 6,
                         out_specs=(tok, tok) + (part,) * 6, check_vma=False)
```

time: 959 us -> 980 us (1.022)
  Pallas kernels: 867 us -> 925 us
  waiting for transfers between devices: 39.9 us -> 3.33 us
    pallas_call x4, Pallas kernels: 867 us -> 925 us  [the longest x1 911 us: block(): pl.pallas_call(block_kernel, grid=(STEPS,), in_specs=[hbm, hbm, vec, vec,...]
    all_to_all x1, waiting for transfers between devices: 39.9 us -> 3.33 us  [local_step(): lax.all_to_all(dx_rest, AXES, 0, 0, tiled=True)]
where the time goes in v2:
time: 980 us
  Pallas kernels  925 us (94%)
  local copies, waits for them, and re-layouts  47.7 us (5%)
    pallas_call x1, Pallas kernels, block(): pl.pallas_call(block_kernel, grid=(STEPS,), in_specs=[hbm, hbm, vec, vec,...  911 us
    slice x1, local copies, waits for them, and re-layouts, local_step(): grads[:3].reshape(3, HEADS, HEAD, MODEL)  34.5 us
  transfers between devices with their start and end apart: 1, of which 1 were waited for; matrix products, arithmetic and copies ran while one was open for 5% of the time, Pallas kernels for 1%

profile of v2, /device:TPU:0, one launch (start us, length us, event | category | flops | bytes accessed | tf_op | source)
XLA Modules:
  0.0 979.9 jit_solution(9968541919556914772)
XLA Ops:
  0.6 911.0 %block.1 = (f32[4,16,128,2048]{3,2,1,0:T(8,128)}, bf16[16,128,2048]{2,1,0:T(8,128)(2,1)}, bf16[16,48,2048]{2,1,0:T(8,128)(2,1)}, bf16[8,2,80,2048]{3,2,1,0:T(8,1...) custom-call(bf16[16,128,2048]{2,1,0:T(8,128)(2,1)} %x_ref.1, ...), custom_call_target="tpu_custom_call" | custom-call | flops 599999971328 | bytes 209715200 | tf_op jit(solution)/shard_map/block/pallas_call | solution.py:625
  911.6 3.4 all-to-all-start
  915.1 11.8 %slice.22 = f32[1,16,128,2048]{3,2,1,0:T(8,128)} slice(f32[4,16,128,2048]{3,2,1,0:T(8,128)} %get-tuple-element.17), slice={[3:4], [0:16], [0:128], [0:2048]} | slice | bytes 33554432 | tf_op jit(solution)/shard_map/slice | solution.py:695
  926.9 0.0 copy-start
  926.9 34.5 %slice.20 = f32[3,16,128,2048]{3,2,1,0:T(8,128)} slice(f32[4,16,128,2048]{3,2,1,0:T(8,128)} %get-tuple-element.17), slice={[0:3], [0:16], [0:128], [0:2048]} | slice | bytes 100663296 | tf_op jit(solution)/shard_map/slice | solution.py:694
  961.4 0.0 copy-done
  961.4 0.7 reshape.47
  962.1 0.6 fusion
  962.7 6.4 settle.3
  969.2 2.8 settle.4.refs_0_
  972.0 3.3 all-to-all-done
  975.3 4.6 settle.5
  (1 shorter events, 0.0 us)
Async XLA Ops:
  911.6 63.7 %all-to-all-start = ((bf16[8,2,80,2048]{3,2,1,0:T(8,128)(2,1)}), bf16[8,2,80,2048]{3,2,1,0:T(8,128)(2,1)}, u32[]{:S(2)}, u32[]{:S(2)}) async-start(bf16[8,2,80,2048]{3,2,1,0:T(8,128)(2,1)} %get-tuple-element.14), calls=%async_computation | async-start | bytes 10485760 | tf_op jit(solution)/shard_map/all_to_all | solution.py:692
  926.9 34.5 %copy-start = (f32[8,2048]{1,0:T(8,128)S(1)}, f32[8,2048]{1,0:T(8,128)}, u32[]{:S(2)}) copy-start(f32[8,2048]{1,0:T(8,128)} %get-tuple-element.16) | copy-start | bytes 196612

commit v3 on v2

--- a/solution.py
+++ b/solution.py
@@ -437,13 +437,9 @@
 
     n = j - PAIRS
     k0, k1 = PAIRS - 2, PAIRS - 1
-    for step, ticks in ((3, ((red.scatter2, 0, k1), (red.forward, 0, k0))),
-                        (5, ((red.scatter2, 1, k1), (red.forward, 1, k0))),
-                        (8, ((red.gather, 0, k1),)),
-                        (9, ((red.own_sent, 0, k0), (red.own_sent, 1, k0), (red.last, 0, k0), (red.last, 1, k0))),
-                        (11, ((red.gather, 1, k1),)),
-                        (18, ((red.forward, 0, k1),)), (22, ((red.forward, 1, k1),)),
-                        (32, ((red.last, 0, k1),)), (36, ((red.last, 1, k1),))):
+    for step, ticks in ((2, ((red.scatter2, 0, k1),)), (5, ((red.gather, 0, k1),)),
+                        (7, ((red.scatter2, 1, k1), (red.forward, 1, k0))), (9, ((red.forward, 0, k0),)),
+                        (27, ((red.forward, 0, k1),)), (36, ((red.gather, 1, k1),)), (38, ((red.last, 1, k0),))):
         @pl.when(n == step)
         def _(ticks=ticks):
             for tick, c, k in ticks:
@@ -588,6 +584,7 @@
 
     @pl.when(j == STEPS - 1)
     def _():
+        red.forward(1, k1)
         copies = [remote(smalls.at[0], smalls.at[o], sm_s.at[o], sm_r.at[o], (0,) + at.peer(o))
                   for o in range(1, SHARDS)]
         for copy in copies:
@@ -598,8 +595,11 @@
         for r in range(1, SHARDS):
             total += smalls[at.slot(r)]
         sum_ref[...] = total
+        for tick, c, k in ((red.last, 0, k0), (red.last, 0, k1), (red.last, 1, k1)):
+            tick(c, k)
         for c in range(SPLIT):
-            red.own_sent(c, k1)
+            for k in (k0, k1):
+                red.own_sent(c, k)
         red.finish()
         others = (SHARDS - 1) * BATCH
         drain(h.at[1:SHARDS], y_s)

time: 980 us -> 950 us (0.969)
  Pallas kernels: 925 us -> 894 us
    pallas_call x1, Pallas kernels: 911 us -> 881 us  [block(): pl.pallas_call(block_kernel, grid=(STEPS,), in_specs=[hbm, hbm, vec, vec,...]
where the time goes in v3:
time: 950 us; the launch traced here: 949 us
  Pallas kernels  894 us (94%)
  local copies, waits for them, and re-layouts  47.7 us (5%)
    pallas_call x1, Pallas kernels, block(): pl.pallas_call(block_kernel, grid=(STEPS,), in_specs=[hbm, hbm, vec, vec,...  881 us
    slice x1, local copies, waits for them, and re-layouts, local_step(): grads[:3].reshape(3, HEADS, HEAD, MODEL)  34.5 us
  transfers between devices with their start and end apart: 1, of which 1 were waited for; matrix products, arithmetic and copies ran while one was open for 5% of the time, Pallas kernels for 1%

profile of v3, /device:TPU:0, one launch (start us, length us, event | category | flops | bytes accessed | tf_op | source)
XLA Modules:
  0.0 949.5 jit_solution(14325511172698349875)
XLA Ops:
  0.6 880.5 %block.1 = (f32[4,16,128,2048]{3,2,1,0:T(8,128)}, bf16[16,128,2048]{2,1,0:T(8,128)(2,1)}, bf16[16,48,2048]{2,1,0:T(8,128)(2,1)}, bf16[8,2,80,2048]{3,2,1,0:T(8,1...) custom-call(bf16[16,128,2048]{2,1,0:T(8,128)(2,1)} %x_ref.1, ...), custom_call_target="tpu_custom_call" | custom-call | flops 599999971328 | bytes 209715200 | tf_op jit(solution)/shard_map/block/pallas_call | solution.py:625
  881.2 3.4 all-to-all-start
  884.6 11.8 %slice.22 = f32[1,16,128,2048]{3,2,1,0:T(8,128)} slice(f32[4,16,128,2048]{3,2,1,0:T(8,128)} %get-tuple-element.17), slice={[3:4], [0:16], [0:128], [0:2048]} | slice | bytes 33554432 | tf_op jit(solution)/shard_map/slice | solution.py:695
  896.4 0.0 copy-start
  896.4 34.5 %slice.20 = f32[3,16,128,2048]{3,2,1,0:T(8,128)} slice(f32[4,16,128,2048]{3,2,1,0:T(8,128)} %get-tuple-element.17), slice={[0:3], [0:16], [0:128], [0:2048]} | slice | bytes 100663296 | tf_op jit(solution)/shard_map/slice | solution.py:694
  930.9 0.0 copy-done
  930.9 0.7 reshape.47
  931.7 0.6 fusion
  932.3 6.4 settle.3
  938.7 2.8 settle.4.refs_0_
  941.5 3.3 all-to-all-done
  944.8 4.6 settle.5
  (1 shorter events, 0.0 us)
Async XLA Ops:
  881.2 63.7 %all-to-all-start = ((bf16[8,2,80,2048]{3,2,1,0:T(8,128)(2,1)}), bf16[8,2,80,2048]{3,2,1,0:T(8,128)(2,1)}, u32[]{:S(2)}, u32[]{:S(2)}) async-start(bf16[8,2,80,2048]{3,2,1,0:T(8,128)(2,1)} %get-tuple-element.14), calls=%async_computation | async-start | bytes 10485760 | tf_op jit(solution)/shard_map/all_to_all | solution.py:692
  896.4 34.5 %copy-start = (f32[8,2048]{1,0:T(8,128)S(1)}, f32[8,2048]{1,0:T(8,128)}, u32[]{:S(2)}) copy-start(f32[8,2048]{1,0:T(8,128)} %get-tuple-element.16) | copy-start | bytes 196612

commit v4 on v3

--- a/solution.py
+++ b/solution.py
@@ -492,6 +492,9 @@
             a_tile(u - 2).start()
             x_tile(u - 2).start()
 
+    def small(o):
+        return remote(smalls.at[0], smalls.at[o], sm_s.at[o], sm_r.at[o], (0,) + at.peer(o))
+
     i = n - STEPS_Y
 
     def d_tiles(i):
@@ -557,8 +560,6 @@
                 for s in range(2):
                     pltpu.make_async_copy(src.at[base + s], dst.at[s], sem.at[s]).wait()
             for s in range(2):
-                u = base + s
-                py, px, pc = at.peer(u)
                 for b in range(BATCH):
                     dh = jnp.concatenate([met[0, 2 * s + b], met[1, 2 * s + b]], axis=1)
                     xf = xbuf[s, b].astype(F32)
@@ -569,7 +570,15 @@
                     smalls[0, 5:6] += jnp.sum(dh, axis=0, keepdims=True)
                     v = dh * lg_ref[...]
                     v = v - jnp.mean(v, axis=-1, keepdims=True) - xn * jnp.mean(v * xn, axis=-1, keepdims=True)
-                    g[u, b] = (lhs_t[s, b].astype(F32) + inv * v).astype(BF16)
+                    g[base + s, b] = (lhs_t[s, b].astype(F32) + inv * v).astype(BF16)
+
+            @pl.when(base == 0)
+            def _():
+                for o in range(1, SHARDS):
+                    small(o).start()
+            for s in range(2):
+                u = base + s
+                py, px, pc = at.peer(u)
                 rest = pl.ds(DIRECT, RUN - DIRECT)
                 pltpu.make_async_copy(g.at[u, :, rest], dxl_ref.at[py * 4 + px * 2 + pc], dxl_s).start()
                 src, dst = g.at[u, :, 0:DIRECT], dxr_ref.at[pl.ds(at.me * BATCH, BATCH)]
@@ -584,19 +593,15 @@
 
     @pl.when(j == STEPS - 1)
     def _():
-        red.forward(1, k1)
-        copies = [remote(smalls.at[0], smalls.at[o], sm_s.at[o], sm_r.at[o], (0,) + at.peer(o))
-                  for o in range(1, SHARDS)]
-        for copy in copies:
-            copy.start()
-        for copy in copies:
-            copy.wait()
+        for tick, c, k in ((red.forward, 1, k1), (red.last, 0, k0), (red.last, 0, k1)):
+            tick(c, k)
+        for o in range(1, SHARDS):
+            small(o).wait()
         total = smalls[at.slot(0)]
         for r in range(1, SHARDS):
             total += smalls[at.slot(r)]
         sum_ref[...] = total
-        for tick, c, k in ((red.last, 0, k0), (red.last, 0, k1), (red.last, 1, k1)):
-            tick(c, k)
+        red.last(1, k1)
         for c in range(SPLIT):
             for k in (k0, k1):
                 red.own_sent(c, k)

time: 950 us -> 946 us (level)
  no operation moved by 1% of the time
where the time goes in v4:
time: 946 us
  Pallas kernels  891 us (94%)
  local copies, waits for them, and re-layouts  47.7 us (5%)
    pallas_call x1, Pallas kernels, block(): pl.pallas_call(block_kernel, grid=(STEPS,), in_specs=[hbm, hbm, vec, vec,...  877 us
    slice x1, local copies, waits for them, and re-layouts, local_step(): grads[:3].reshape(3, HEADS, HEAD, MODEL)  34.5 us
  transfers between devices with their start and end apart: 1, of which 1 were waited for; matrix products, arithmetic and copies ran while one was open for 5% of the time, Pallas kernels for 1%

profile of v4, /device:TPU:0, one launch (start us, length us, event | category | flops | bytes accessed | tf_op | source)
XLA Modules:
  0.0 945.9 jit_solution(7781801568310353269)
XLA Ops:
  0.6 876.9 %block.1 = (f32[4,16,128,2048]{3,2,1,0:T(8,128)}, bf16[16,128,2048]{2,1,0:T(8,128)(2,1)}, bf16[16,48,2048]{2,1,0:T(8,128)(2,1)}, bf16[8,2,80,2048]{3,2,1,0:T(8,1...) custom-call(bf16[16,128,2048]{2,1,0:T(8,128)(2,1)} %x_ref.1, ...), custom_call_target="tpu_custom_call" | custom-call | flops 599999971328 | bytes 209715200 | tf_op jit(solution)/shard_map/block/pallas_call | solution.py:630
  877.6 3.4 all-to-all-start
  881.0 11.8 %slice.22 = f32[1,16,128,2048]{3,2,1,0:T(8,128)} slice(f32[4,16,128,2048]{3,2,1,0:T(8,128)} %get-tuple-element.17), slice={[3:4], [0:16], [0:128], [0:2048]} | slice | bytes 33554432 | tf_op jit(solution)/shard_map/slice | solution.py:700
  892.8 0.0 copy-start
  892.8 34.5 %slice.20 = f32[3,16,128,2048]{3,2,1,0:T(8,128)} slice(f32[4,16,128,2048]{3,2,1,0:T(8,128)} %get-tuple-element.17), slice={[0:3], [0:16], [0:128], [0:2048]} | slice | bytes 100663296 | tf_op jit(solution)/shard_map/slice | solution.py:699
  927.3 0.0 copy-done
  927.4 0.7 reshape.47
  928.1 0.6 fusion
  928.7 6.4 settle.3
  935.1 2.8 settle.4.refs_0_
  937.9 3.3 all-to-all-done
  941.2 4.6 settle.5
  (1 shorter events, 0.0 us)
Async XLA Ops:
  877.6 63.7 %all-to-all-start = ((bf16[8,2,80,2048]{3,2,1,0:T(8,128)(2,1)}), bf16[8,2,80,2048]{3,2,1,0:T(8,128)(2,1)}, u32[]{:S(2)}, u32[]{:S(2)}) async-start(bf16[8,2,80,2048]{3,2,1,0:T(8,128)(2,1)} %get-tuple-element.14), calls=%async_computation | async-start | bytes 10485760 | tf_op jit(solution)/shard_map/all_to_all | solution.py:697
  892.8 34.5 %copy-start = (f32[8,2048]{1,0:T(8,128)S(1)}, f32[8,2048]{1,0:T(8,128)}, u32[]{:S(2)}) copy-start(f32[8,2048]{1,0:T(8,128)} %get-tuple-element.16) | copy-start | bytes 196612

commit v5 on v4

--- a/solution.py
+++ b/solution.py
@@ -231,8 +231,8 @@
 
 
 def pair_step(j, at, red, x_ref, g_ref, lg_ref, lb_ref, w_ref, wo_ref, b_ref, xt_ref, gt_ref, d_ref,
-              h, g, w, wo, qkv, da, lhs_t, kt, vt, dk_acc, dv_acc, away, met, made, smalls,
-              w_s, wo_s, x_s, x_r, g_s, g_r, keep_s, met_s, met_r, made_s):
+              h, g, w, wo, qkv, da, lhs_t, kt, vt, dk_acc, dv_acc, away, met, made, smalls, first,
+              w_s, wo_s, x_s, x_r, g_s, g_r, keep_s, met_s, met_r, made_s, f_in, f_s, f_r):
     par = j % 2
     part = red.part
     slots = [at.slot(r) for r in range(SHARDS)]
@@ -257,6 +257,9 @@
             return pltpu.make_async_copy(row, g.at[0, b], g_r.at[b, 0])
         return remote(row, g.at[u, b], g_s.at[b, u], g_r.at[b, u], (0, py, px, pc))
 
+    def send_first(u):
+        return remote(first.at[u], da.at[0, u, 1], f_s.at[u], f_r.at[u], (0,) + at.peer(u))
+
     def g_landed(b, u):
         drain(g.at[u, b], g_r.at[b, u])
 
@@ -266,11 +269,29 @@
         order = (0, 3, 1, 2, 7, 5, 6, 4)
         for u in order:
             send_x(u).start()
-        for b in range(BATCH):
-            for u in order:
-                send_g(b, u).start()
         for copy in weights(0):
             copy.start()
+        for u in order:
+            send_g(0, u).start()
+
+        weights(0)[1].wait()
+        for u in range(0, SHARDS, 4):
+            tiles = []
+            for n in range(4):
+                py, px, pc = at.peer(u + n)
+                row = (py * 4 + px * 2 + pc) * BATCH + 1
+                tiles.append(pltpu.make_async_copy(g_ref.at[row], lhs_t.at[n // 2, n % 2], f_in.at[n]))
+            for copy in tiles:
+                copy.start()
+            for copy in tiles:
+                copy.wait()
+            r = lax.dot_general(lhs_t[...].reshape(4 * RUN, MODEL), wo[0, 0], NT, preferred_element_type=F32)
+            first[u:u + 4] = r.astype(BF16).reshape(4, RUN, LANES)
+        da[0, 0, 1] = first[0]
+        for u in order[1:]:
+            send_first(u).start()
+        for u in order:
+            send_g(1, u).start()
 
         @pl.loop(0, SHARDS)
         def _(u):
@@ -288,8 +309,7 @@
 
     @pl.when(par == 0)
     def _():
-        for copy in weights(q):
-            copy.wait()
+        weights(q)[0].wait()
         step = 4
         for r in range(0, SHARDS, step):
             hr = h[r:r + step].reshape(step * BATCH * RUN, MODEL)
@@ -321,6 +341,10 @@
         for u in range(SHARDS):
             g_landed(0, u)
 
+    @pl.when((par == 0) & (j > 0))
+    def _():
+        weights(q)[1].wait()
+
     @pl.when(par == 0)
     def _():
         project_da(0)
@@ -343,11 +367,10 @@
 
     @pl.when(j == 0)
     def _():
-        for u in range(SHARDS):
-            g_landed(1, u)
-        pltpu.make_async_copy(g, gt_ref, keep_s).start()
-
-    @pl.when(par == 0)
+        for u in range(1, SHARDS):
+            drain(da.at[0, u, 1], f_r.at[u])
+
+    @pl.when((par == 0) & (j > 0))
     def _():
         project_da(1)
 
@@ -366,6 +389,7 @@
     def _():
         for u in range(1, SHARDS):
             send_x(u).wait_send()
+            send_first(u).wait_send()
             for b in range(BATCH):
                 send_g(b, u).wait_send()
         pltpu.make_async_copy(g, gt_ref, keep_s).wait()
@@ -376,15 +400,20 @@
             smalls[0, 3:4] += jnp.sum(g[u].reshape(BATCH * RUN, MODEL).astype(F32), axis=0, keepdims=True)
         smalls[0, 4:8] = jnp.zeros((4, MODEL), F32)
 
-    def weight_grad(dst, c, side):
-        width = HALF // SPLIT
+    width = HALF // SPLIT
+
+    def columns(ref, c, side):
         cols = pl.ds(pl.multiple_of(side * HALF + c * width, width), width)
-        hc = h[:, :, :, cols].reshape(TOKENS, width)
-        gc = g[:, :, :, cols].reshape(TOKENS, width)
-        lhs = lhs_t[...].reshape(4 * LANES, TOKENS)
-        r = lax.dot_general(lhs[0:3 * LANES], hc, NN, preferred_element_type=F32)
+        return ref[:, :, :, cols].reshape(TOKENS, width)
+
+    def grad_qkv(dst, c, side):
+        lhs = lhs_t[...].reshape(4 * LANES, TOKENS)[0:3 * LANES]
+        r = lax.dot_general(lhs, columns(h, c, side), NN, preferred_element_type=F32)
         dst[0:3, :, red.cols(c)] = r.reshape(3, LANES, width)
-        dst[3, :, red.cols(c)] = lax.dot_general(lhs[3 * LANES:], gc, NN, preferred_element_type=F32)
+
+    def grad_out(dst, c, side):
+        lhs = lhs_t[...].reshape(4 * LANES, TOKENS)[3 * LANES:]
+        dst[3, :, red.cols(c)] = lax.dot_general(lhs, columns(g, c, side), NN, preferred_element_type=F32)
 
     def meet(c, k):
         return pair_meet(red, at, away, met, met_s, met_r, c, k)
@@ -393,7 +422,14 @@
         @pl.when(j >= 1)
         def _():
             meet(c, j - 1).wait_send()
-        weight_grad(away, c, 1 - at.core)
+        grad_qkv(away, c, 1 - at.core)
+        if c == 0:
+            @pl.when(j == 0)
+            def _():
+                for u in range(SHARDS):
+                    g_landed(1, u)
+                pltpu.make_async_copy(g, gt_ref, keep_s).start()
+        grad_out(away, c, 1 - at.core)
         meet(c, j).start()
         if c == 0:
             @pl.when(j >= 1)
@@ -409,12 +445,17 @@
         @pl.when(j >= 2)
         def _():
             red.last(c, j - 2)
-        weight_grad(part.at[par], c, at.core)
+        grad_qkv(part.at[par], c, at.core)
+        grad_out(part.at[par], c, at.core)
         meet(c, j).wait_recv()
         cols = red.cols(c)
         part[par, :, :, cols] = part[par, :, :, cols] + met[par, :, :, cols]
         red.rs1(c, j).start()
 
+    @pl.when(j == 0)
+    def _():
+        project_da(1)
+
     @pl.when(j >= 1)
     def _():
         red.gather(1, j - 1)
@@ -422,8 +463,8 @@
 
 def block_kernel(x_ref, g_ref, lg_ref, lb_ref, w_ref, wo_ref, b_ref, bo_ref,
                  out_ref, y_ref, dxr_ref, dxl_ref, sum_ref, xt_ref, gt_ref, d_ref,
-                 h, g, w, wo, qkv, da, lhs_t, kt, vt, dk_acc, dv_acc, away, met, made, smalls,
-                 w_s, wo_s, x_s, x_r, g_s, g_r, keep_s, met_s, met_r, made_s, a_s, xb_s, big_s, tile_s, lt_s,
+                 h, g, w, wo, qkv, da, lhs_t, kt, vt, dk_acc, dv_acc, away, met, made, smalls, first,
+                 w_s, wo_s, x_s, x_r, g_s, g_r, keep_s, met_s, met_r, made_s, f_in, f_s, f_r, a_s, xb_s, big_s, tile_s, lt_s,
                  y_s, y_r, yk_s, dx_s, dx_r, dxk_s, dxl_s, sm_s, sm_r, part, recv1, recv2, *sems):
     j = pl.program_id(0)
     at = Place()
@@ -432,8 +473,8 @@
     @pl.when(j < PAIRS)
     def _():
         pair_step(j, at, red, x_ref, g_ref, lg_ref, lb_ref, w_ref, wo_ref, b_ref, xt_ref, gt_ref, d_ref,
-                  h, g, w, wo, qkv, da, lhs_t, kt, vt, dk_acc, dv_acc, away, met, made, smalls,
-                  w_s, wo_s, x_s, x_r, g_s, g_r, keep_s, met_s, met_r, made_s)
+                  h, g, w, wo, qkv, da, lhs_t, kt, vt, dk_acc, dv_acc, away, met, made, smalls, first,
+                  w_s, wo_s, x_s, x_r, g_s, g_r, keep_s, met_s, met_r, made_s, f_in, f_s, f_r)
 
     n = j - PAIRS
     k0, k1 = PAIRS - 2, PAIRS - 1
@@ -646,9 +687,10 @@
             pltpu.VMEM((SEQ, LANES), F32), pltpu.VMEM((SEQ, LANES), F32),
             pltpu.VMEM((4, LANES, HALF), F32), pltpu.VMEM((2, 4, LANES, HALF), F32),
             pltpu.VMEM((2, 4) + heads, BF16),
-            pltpu.VMEM((SHARDS, 8, MODEL), F32),
+            pltpu.VMEM((SHARDS, 8, MODEL), F32), pltpu.VMEM((SHARDS, RUN, LANES), BF16),
             two, two, DMA((SHARDS,)), DMA((SHARDS,)), DMA((BATCH, SHARDS)), DMA((BATCH, SHARDS)), DMA,
-            DMA((SPLIT,)), DMA((SPLIT, 2)), two, two, two, DMA, DMA((4,)), two,
+            DMA((SPLIT,)), DMA((SPLIT, 2)), two, DMA((4,)), DMA((SHARDS,)), DMA((SHARDS,)),
+            two, two, DMA, DMA((4,)), two,
             DMA, DMA, DMA, DMA, DMA, DMA, DMA, DMA((SHARDS,)), DMA((SHARDS,))]
         + reduce_scratch(SPLIT),
         name="block",

time: 946 us -> 942 us (level)
  no operation moved by 1% of the time
where the time goes in v5:
time: 942 us
  Pallas kernels  887 us (94%)
  local copies, waits for them, and re-layouts  47.7 us (5%)
    pallas_call x1, Pallas kernels, block(): pl.pallas_call(block_kernel, grid=(STEPS,), in_specs=[hbm, hbm, vec, vec,...  873 us
    slice x1, local copies, waits for them, and re-layouts, local_step(): grads[:3].reshape(3, HEADS, HEAD, MODEL)  34.5 us
  transfers between devices with their start and end apart: 1, of which 1 were waited for; matrix products, arithmetic and copies ran while one was open for 5% of the time, Pallas kernels for 1%

profile of v5, /device:TPU:0, one launch (start us, length us, event | category | flops | bytes accessed | tf_op | source)
XLA Modules:
  0.0 941.7 jit_solution(8291697592281911037)
XLA Ops:
  0.6 872.8 %block.1 = (f32[4,16,128,2048]{3,2,1,0:T(8,128)}, bf16[16,128,2048]{2,1,0:T(8,128)(2,1)}, bf16[16,48,2048]{2,1,0:T(8,128)(2,1)}, bf16[8,2,80,2048]{3,2,1,0:T(8,1...) custom-call(bf16[16,128,2048]{2,1,0:T(8,128)(2,1)} %x_ref.1, ...), custom_call_target="tpu_custom_call" | custom-call | flops 599999971328 | bytes 209715200 | tf_op jit(solution)/shard_map/block/pallas_call | solution.py:671
  873.4 3.4 all-to-all-start
  876.8 11.8 %slice.22 = f32[1,16,128,2048]{3,2,1,0:T(8,128)} slice(f32[4,16,128,2048]{3,2,1,0:T(8,128)} %get-tuple-element.17), slice={[3:4], [0:16], [0:128], [0:2048]} | slice | bytes 33554432 | tf_op jit(solution)/shard_map/slice | solution.py:742
  888.6 0.0 copy-start
  888.6 34.5 %slice.20 = f32[3,16,128,2048]{3,2,1,0:T(8,128)} slice(f32[4,16,128,2048]{3,2,1,0:T(8,128)} %get-tuple-element.17), slice={[0:3], [0:16], [0:128], [0:2048]} | slice | bytes 100663296 | tf_op jit(solution)/shard_map/slice | solution.py:741
  923.2 0.0 copy-done
  923.2 0.7 reshape.47
  923.9 0.6 fusion
  924.5 6.4 settle.3
  930.9 2.8 settle.4.refs_0_
  933.7 3.3 all-to-all-done
  937.1 4.6 settle.5
  (1 shorter events, 0.0 us)
Async XLA Ops:
  873.4 63.7 %all-to-all-start = ((bf16[8,2,80,2048]{3,2,1,0:T(8,128)(2,1)}), bf16[8,2,80,2048]{3,2,1,0:T(8,128)(2,1)}, u32[]{:S(2)}, u32[]{:S(2)}) async-start(bf16[8,2,80,2048]{3,2,1,0:T(8,128)(2,1)} %get-tuple-element.14), calls=%async_computation | async-start | bytes 10485760 | tf_op jit(solution)/shard_map/all_to_all | solution.py:739
  888.6 34.5 %copy-start = (f32[8,2048]{1,0:T(8,128)S(1)}, f32[8,2048]{1,0:T(8,128)}, u32[]{:S(2)}) copy-start(f32[8,2048]{1,0:T(8,128)} %get-tuple-element.16) | copy-start | bytes 196612

commit v6 on v5

--- a/solution.py
+++ b/solution.py
@@ -354,9 +354,11 @@
         def _():
             red.scatter2(c, j - 1)
 
-        @pl.when(j >= 2)
-        def _():
-            red.forward(c, j - 2)
+        if c == 0:
+            @pl.when(j >= 2)
+            def _():
+                for piece in range(SPLIT):
+                    red.forward(piece, j - 2)
 
     @pl.when(j >= 2)
     def _():
@@ -440,13 +442,19 @@
     def _():
         for c in range(SPLIT):
             red.own_sent(c, j - 2)
+        red.last(0, j - 2)
 
     for c in range(SPLIT):
-        @pl.when(j >= 2)
-        def _():
-            red.last(c, j - 2)
         grad_qkv(part.at[par], c, at.core)
         grad_out(part.at[par], c, at.core)
+        if c == 1:
+            @pl.when(j >= 1)
+            def _():
+                red.gather(1, j - 1)
+
+            @pl.when(j >= 2)
+            def _():
+                red.last(1, j - 2)
         meet(c, j).wait_recv()
         cols = red.cols(c)
         part[par, :, :, cols] = part[par, :, :, cols] + met[par, :, :, cols]
@@ -455,10 +463,6 @@
     @pl.when(j == 0)
     def _():
         project_da(1)
-
-    @pl.when(j >= 1)
-    def _():
-        red.gather(1, j - 1)
 
 
 def block_kernel(x_ref, g_ref, lg_ref, lb_ref, w_ref, wo_ref, b_ref, bo_ref,

time: 942 us -> 939 us (level)
  no operation moved by 1% of the time
where the time goes in v6:
time: 939 us; the launch traced here: 938 us
  Pallas kernels  883 us (94%)
  local copies, waits for them, and re-layouts  47.7 us (5%)
    pallas_call x1, Pallas kernels, block(): pl.pallas_call(block_kernel, grid=(STEPS,), in_specs=[hbm, hbm, vec, vec,...  869 us
    slice x1, local copies, waits for them, and re-layouts, local_step(): grads[:3].reshape(3, HEADS, HEAD, MODEL)  34.5 us
  transfers between devices with their start and end apart: 1, of which 1 were waited for; matrix products, arithmetic and copies ran while one was open for 5% of the time, Pallas kernels for 1%

profile of v6, /device:TPU:0, one launch (start us, length us, event | category | flops | bytes accessed | tf_op | source)
XLA Modules:
  0.0 938.1 jit_solution(313754229242871330)
XLA Ops:
  0.6 869.1 %block.1 = (f32[4,16,128,2048]{3,2,1,0:T(8,128)}, bf16[16,128,2048]{2,1,0:T(8,128)(2,1)}, bf16[16,48,2048]{2,1,0:T(8,128)(2,1)}, bf16[8,2,80,2048]{3,2,1,0:T(8,1...) custom-call(bf16[16,128,2048]{2,1,0:T(8,128)(2,1)} %x_ref.1, ...), custom_call_target="tpu_custom_call" | custom-call | flops 599999971328 | bytes 209715200 | tf_op jit(solution)/shard_map/block/pallas_call | solution.py:675
  869.8 3.4 all-to-all-start
  873.2 11.8 %slice.22 = f32[1,16,128,2048]{3,2,1,0:T(8,128)} slice(f32[4,16,128,2048]{3,2,1,0:T(8,128)} %get-tuple-element.17), slice={[3:4], [0:16], [0:128], [0:2048]} | slice | bytes 33554432 | tf_op jit(solution)/shard_map/slice | solution.py:746
  885.0 0.0 copy-start
  885.0 34.5 %slice.20 = f32[3,16,128,2048]{3,2,1,0:T(8,128)} slice(f32[4,16,128,2048]{3,2,1,0:T(8,128)} %get-tuple-element.17), slice={[0:3], [0:16], [0:128], [0:2048]} | slice | bytes 100663296 | tf_op jit(solution)/shard_map/slice | solution.py:745
  919.5 0.0 copy-done
  919.6 0.7 reshape.47
  920.3 0.6 fusion
  920.9 6.4 settle.3
  927.3 2.8 settle.4.refs_0_
  930.1 3.3 all-to-all-done
  933.4 4.6 settle.5
  (1 shorter events, 0.0 us)
Async XLA Ops:
  869.8 63.7 %all-to-all-start = ((bf16[8,2,80,2048]{3,2,1,0:T(8,128)(2,1)}), bf16[8,2,80,2048]{3,2,1,0:T(8,128)(2,1)}, u32[]{:S(2)}, u32[]{:S(2)}) async-start(bf16[8,2,80,2048]{3,2,1,0:T(8,128)(2,1)} %get-tuple-element.14), calls=%async_computation | async-start | bytes 10485760 | tf_op jit(solution)/shard_map/all_to_all | solution.py:743
  885.0 34.5 %copy-start = (f32[8,2048]{1,0:T(8,128)S(1)}, f32[8,2048]{1,0:T(8,128)}, u32[]{:S(2)}) copy-start(f32[8,2048]{1,0:T(8,128)} %get-tuple-element.16) | copy-start | bytes 196612

commit v7 on v6

--- a/solution.py
+++ b/solution.py
@@ -68,7 +68,7 @@
         self.at, self.out, self.split = at, out_ref, split
         self.part, self.recv1, self.recv2 = part, recv1, recv2
         (self.rs1_s, self.rs1_r, self.rs2_s, self.rs2_r, self.ag_s, self.n1_r, self.n2_r, self.fw_r,
-         self.fw_s, self.core_s, self.core_r) = sems
+         self.fw_s, self.core_s, self.core_r, self.half_s, self.half_r) = sems
 
     def cols(self, c):
         width = HALF // self.split
@@ -82,6 +82,11 @@
         s, away = k % 2, pl.ds((1 - self.at.c1) * 2, 2)
         return remote(self.part.at[s, away, :, self.cols(c)], self.recv1.at[s, :, :, self.cols(c)],
                       self.rs1_s.at[c, s], self.rs1_r.at[c, s], self.at.n1)
+
+    def rs1_half(self, c, n):
+        sems = (self.rs1_s.at[c, 0], self.rs1_r.at[c, 0]) if n == 0 else (self.half_s.at[c], self.half_r.at[c])
+        return remote(self.part.at[0, (1 - self.at.c1) * 2 + n, :, self.cols(c)], self.recv1.at[0, n, :, self.cols(c)],
+                      *sems, self.at.n1)
 
     def rs2(self, c, k):
         s = k % 2
@@ -105,7 +110,16 @@
 
     def scatter2(self, c, k):
         s, keep, cols = k % 2, pl.ds(self.at.c1 * 2, 2), self.cols(c)
-        self.rs1(c, k).wait()
+
+        @pl.when(k == 0)
+        def _():
+            for n in range(2):
+                self.rs1_half(c, n).wait()
+
+        @pl.when(k > 0)
+        def _():
+            self.rs1(c, k).wait()
+
         self.part[s, keep, :, cols] = self.part[s, keep, :, cols] + self.recv1[s, :, :, cols]
         self.rs2(c, k).start()
 
@@ -147,7 +161,8 @@
 def reduce_scratch(split):
     two = DMA((split, 2))
     return [pltpu.VMEM((2, 4, LANES, HALF), F32), pltpu.VMEM((2, 2, LANES, HALF), F32),
-            pltpu.VMEM((2, LANES, HALF), F32), two, two, two, two, DMA((split, 2, 4)), two, two, two, DMA, DMA, DMA]
+            pltpu.VMEM((2, LANES, HALF), F32), two, two, two, two, DMA((split, 2, 4)), two, two, two, DMA, DMA, DMA,
+            DMA((split,)), DMA((split,))]
 
 
 def fold(v, op):
@@ -232,7 +247,7 @@
 
 def pair_step(j, at, red, x_ref, g_ref, lg_ref, lb_ref, w_ref, wo_ref, b_ref, xt_ref, gt_ref, d_ref,
               h, g, w, wo, qkv, da, lhs_t, kt, vt, dk_acc, dv_acc, away, met, made, smalls, first,
-              w_s, wo_s, x_s, x_r, g_s, g_r, keep_s, met_s, met_r, made_s, f_in, f_s, f_r):
+              w_s, wo_s, x_s, x_r, g_s, g_r, keep_s, met_s, met_r, made_s, f_in, f_s, f_r, mo_s, mo_r):
     par = j % 2
     part = red.part
     slots = [at.slot(r) for r in range(SHARDS)]
@@ -420,55 +435,75 @@
     def meet(c, k):
         return pair_meet(red, at, away, met, met_s, met_r, c, k)
 
-    for c in range(SPLIT):
-        @pl.when(j >= 1)
-        def _():
-            meet(c, j - 1).wait_send()
-        grad_qkv(away, c, 1 - at.core)
-        if c == 0:
-            @pl.when(j == 0)
-            def _():
+    def meet_first(c, n):
+        rows, cols = pl.ds(3 * n, 3 - 2 * n), red.cols(c)
+        sems = (met_s.at[c], met_r.at[c, 0]) if n == 0 else (mo_s.at[c], mo_r.at[c])
+        return remote(away.at[rows, :, cols], met.at[0, rows, :, cols], *sems, at.mate)
+
+    @pl.when(j == 0)
+    def _():
+        for n, grad in enumerate((grad_qkv, grad_out)):
+            if n == 1:
                 for u in range(SHARDS):
                     g_landed(1, u)
                 pltpu.make_async_copy(g, gt_ref, keep_s).start()
-        grad_out(away, c, 1 - at.core)
-        meet(c, j).start()
-        if c == 0:
-            @pl.when(j >= 1)
-            def _():
+            for c in range(SPLIT):
+                grad(away, c, 1 - at.core)
+                meet_first(c, n).start()
+            for c in range(SPLIT):
+                grad(part.at[0], c, at.core)
+            for c in range(SPLIT):
+                meet_first(c, n).wait_recv()
+                rows, cols = slice(3 * n, 3 + n), red.cols(c)
+                part[0, rows, :, cols] = part[0, rows, :, cols] + met[0, rows, :, cols]
+                red.rs1_half(c, n).start()
+        project_da(1)
+
+    @pl.when(j == 1)
+    def _():
+        for c in range(SPLIT):
+            for n in range(2):
+                meet_first(c, n).wait_send()
+
+    @pl.when(j >= 2)
+    def _():
+        for c in range(SPLIT):
+            meet(c, j - 1).wait_send()
+
+    @pl.when(j >= 1)
+    def _():
+        for c in range(SPLIT):
+            grad_qkv(away, c, 1 - at.core)
+            grad_out(away, c, 1 - at.core)
+            meet(c, j).start()
+            if c == 0:
                 red.gather(0, j - 1)
 
-    @pl.when(j >= 2)
-    def _():
+        @pl.when(j >= 2)
+        def _():
+            for c in range(SPLIT):
+                red.own_sent(c, j - 2)
+            red.last(0, j - 2)
+
         for c in range(SPLIT):
-            red.own_sent(c, j - 2)
-        red.last(0, j - 2)
-
-    for c in range(SPLIT):
-        grad_qkv(part.at[par], c, at.core)
-        grad_out(part.at[par], c, at.core)
-        if c == 1:
-            @pl.when(j >= 1)
-            def _():
+            grad_qkv(part.at[par], c, at.core)
+            grad_out(part.at[par], c, at.core)
+            if c == 1:
                 red.gather(1, j - 1)
 
-            @pl.when(j >= 2)
-            def _():
-                red.last(1, j - 2)
-        meet(c, j).wait_recv()
-        cols = red.cols(c)
-        part[par, :, :, cols] = part[par, :, :, cols] + met[par, :, :, cols]
-        red.rs1(c, j).start()
-
-    @pl.when(j == 0)
-    def _():
-        project_da(1)
+                @pl.when(j >= 2)
+                def _():
+                    red.last(1, j - 2)
+            meet(c, j).wait_recv()
+            cols = red.cols(c)
+            part[par, :, :, cols] = part[par, :, :, cols] + met[par, :, :, cols]
+            red.rs1(c, j).start()
 
 
 def block_kernel(x_ref, g_ref, lg_ref, lb_ref, w_ref, wo_ref, b_ref, bo_ref,
                  out_ref, y_ref, dxr_ref, dxl_ref, sum_ref, xt_ref, gt_ref, d_ref,
                  h, g, w, wo, qkv, da, lhs_t, kt, vt, dk_acc, dv_acc, away, met, made, smalls, first,
-                 w_s, wo_s, x_s, x_r, g_s, g_r, keep_s, met_s, met_r, made_s, f_in, f_s, f_r, a_s, xb_s, big_s, tile_s, lt_s,
+                 w_s, wo_s, x_s, x_r, g_s, g_r, keep_s, met_s, met_r, made_s, f_in, f_s, f_r, mo_s, mo_r, a_s, xb_s, big_s, tile_s, lt_s,
                  y_s, y_r, yk_s, dx_s, dx_r, dxk_s, dxl_s, sm_s, sm_r, part, recv1, recv2, *sems):
     j = pl.program_id(0)
     at = Place()
@@ -478,7 +513,7 @@
     def _():
         pair_step(j, at, red, x_ref, g_ref, lg_ref, lb_ref, w_ref, wo_ref, b_ref, xt_ref, gt_ref, d_ref,
                   h, g, w, wo, qkv, da, lhs_t, kt, vt, dk_acc, dv_acc, away, met, made, smalls, first,
-                  w_s, wo_s, x_s, x_r, g_s, g_r, keep_s, met_s, met_r, made_s, f_in, f_s, f_r)
+                  w_s, wo_s, x_s, x_r, g_s, g_r, keep_s, met_s, met_r, made_s, f_in, f_s, f_r, mo_s, mo_r)
 
     n = j - PAIRS
     k0, k1 = PAIRS - 2, PAIRS - 1
@@ -604,18 +639,20 @@
             for src, dst, sem in tiles:
                 for s in range(2):
                     pltpu.make_async_copy(src.at[base + s], dst.at[s], sem.at[s]).wait()
-            for s in range(2):
-                for b in range(BATCH):
-                    dh = jnp.concatenate([met[0, 2 * s + b], met[1, 2 * s + b]], axis=1)
-                    xf = xbuf[s, b].astype(F32)
-                    cen = xf - jnp.mean(xf, axis=-1, keepdims=True)
-                    inv = lax.rsqrt(jnp.mean(cen * cen, axis=-1, keepdims=True) + LN_EPS)
-                    xn = cen * inv
-                    smalls[0, 4:5] += jnp.sum(dh * xn, axis=0, keepdims=True)
-                    smalls[0, 5:6] += jnp.sum(dh, axis=0, keepdims=True)
-                    v = dh * lg_ref[...]
-                    v = v - jnp.mean(v, axis=-1, keepdims=True) - xn * jnp.mean(v * xn, axis=-1, keepdims=True)
-                    g[base + s, b] = (lhs_t[s, b].astype(F32) + inv * v).astype(BF16)
+
+            @pl.loop(0, 2 * BATCH)
+            def _(tile):
+                s, b = tile // BATCH, tile % BATCH
+                dh = jnp.concatenate([met[0, tile], met[1, tile]], axis=1)
+                xf = xbuf[s, b].astype(F32)
+                cen = xf - jnp.mean(xf, axis=-1, keepdims=True)
+                inv = lax.rsqrt(jnp.mean(cen * cen, axis=-1, keepdims=True) + LN_EPS)
+                xn = cen * inv
+                smalls[0, 4:5] += jnp.sum(dh * xn, axis=0, keepdims=True)
+                smalls[0, 5:6] += jnp.sum(dh, axis=0, keepdims=True)
+                v = dh * lg_ref[...]
+                v = v - jnp.mean(v, axis=-1, keepdims=True) - xn * jnp.mean(v * xn, axis=-1, keepdims=True)
+                g[base + s, b] = (lhs_t[s, b].astype(F32) + inv * v).astype(BF16)
 
             @pl.when(base == 0)
             def _():
@@ -694,6 +731,7 @@
             pltpu.VMEM((SHARDS, 8, MODEL), F32), pltpu.VMEM((SHARDS, RUN, LANES), BF16),
             two, two, DMA((SHARDS,)), DMA((SHARDS,)), DMA((BATCH, SHARDS)), DMA((BATCH, SHARDS)), DMA,
             DMA((SPLIT,)), DMA((SPLIT, 2)), two, DMA((4,)), DMA((SHARDS,)), DMA((SHARDS,)),
+            DMA((SPLIT,)), DMA((SPLIT,)),
             two, two, DMA, DMA((4,)), two,
             DMA, DMA, DMA, DMA, DMA, DMA, DMA, DMA((SHARDS,)), DMA((SHARDS,))]
         + reduce_scratch(SPLIT),

time: 939 us -> 934 us (level)
  no operation moved by 1% of the time
where the time goes in v7:
time: 934 us
  Pallas kernels  878 us (94%)
  local copies, waits for them, and re-layouts  47.7 us (5%)
    pallas_call x1, Pallas kernels, block(): pl.pallas_call(block_kernel, grid=(STEPS,), in_specs=[hbm, hbm, vec, vec,...  865 us
    slice x1, local copies, waits for them, and re-layouts, local_step(): grads[:3].reshape(3, HEADS, HEAD, MODEL)  34.5 us
  transfers between devices with their start and end apart: 1, of which 1 were waited for; matrix products, arithmetic and copies ran while one was open for 5% of the time, Pallas kernels for 1%

profile of v7, /device:TPU:0, one launch (start us, length us, event | category | flops | bytes accessed | tf_op | source)
XLA Modules:
  0.0 933.5 jit_solution(12958351455059812431)
XLA Ops:
  0.6 864.6 %block.1 = (f32[4,16,128,2048]{3,2,1,0:T(8,128)}, bf16[16,128,2048]{2,1,0:T(8,128)(2,1)}, bf16[16,48,2048]{2,1,0:T(8,128)(2,1)}, bf16[8,2,80,2048]{3,2,1,0:T(8,1...) custom-call(bf16[16,128,2048]{2,1,0:T(8,128)(2,1)} %x_ref.1, ...), custom_call_target="tpu_custom_call" | custom-call | flops 599999971328 | bytes 209715200 | tf_op jit(solution)/shard_map/block/pallas_call | solution.py:712
  865.2 3.4 all-to-all-start
  868.7 11.8 %slice.22 = f32[1,16,128,2048]{3,2,1,0:T(8,128)} slice(f32[4,16,128,2048]{3,2,1,0:T(8,128)} %get-tuple-element.17), slice={[3:4], [0:16], [0:128], [0:2048]} | slice | bytes 33554432 | tf_op jit(solution)/shard_map/slice | solution.py:784
  880.5 0.0 copy-start
  880.5 34.5 %slice.20 = f32[3,16,128,2048]{3,2,1,0:T(8,128)} slice(f32[4,16,128,2048]{3,2,1,0:T(8,128)} %get-tuple-element.17), slice={[0:3], [0:16], [0:128], [0:2048]} | slice | bytes 100663296 | tf_op jit(solution)/shard_map/slice | solution.py:783
  915.0 0.0 copy-done
  915.0 0.7 reshape.47
  915.7 0.6 fusion
  916.4 6.4 settle.3
  922.8 2.8 settle.4.refs_0_
  925.6 3.3 all-to-all-done
  928.9 4.6 settle.5
  (1 shorter events, 0.0 us)
Async XLA Ops:
  865.2 63.7 %all-to-all-start = ((bf16[8,2,80,2048]{3,2,1,0:T(8,128)(2,1)}), bf16[8,2,80,2048]{3,2,1,0:T(8,128)(2,1)}, u32[]{:S(2)}, u32[]{:S(2)}) async-start(bf16[8,2,80,2048]{3,2,1,0:T(8,128)(2,1)} %get-tuple-element.14), calls=%async_computation | async-start | bytes 10485760 | tf_op jit(solution)/shard_map/all_to_all | solution.py:781
  880.5 34.5 %copy-start = (f32[8,2048]{1,0:T(8,128)S(1)}, f32[8,2048]{1,0:T(8,128)}, u32[]{:S(2)}) copy-start(f32[8,2048]{1,0:T(8,128)} %get-tuple-element.16) | copy-start | bytes 196612

commit v8 on v7

--- a/solution.py
+++ b/solution.py
@@ -743,18 +743,51 @@
 
 def settle_kernel(src_ref, *refs):
     *_, dst_ref, buf, in_s, out_s = refs
-    first = dst_ref.shape[1] - src_ref.shape[1] if len(refs) == 5 else 0
-    at = pl.ds(first, src_ref.shape[1])
-    rows = lambda i: pl.ds(i * BATCH, BATCH)
-    get = [pltpu.make_async_copy(src_ref.at[rows(i)], buf.at[rows(i)], in_s.at[i]) for i in range(SHARDS)]
-    put = [pltpu.make_async_copy(buf.at[rows(i)], dst_ref.at[rows(i), at], out_s.at[i]) for i in range(SHARDS)]
+    at = pl.ds(dst_ref.shape[1] - src_ref.shape[1] if len(refs) == 5 else 0, src_ref.shape[1])
+    count = src_ref.shape[0]
+    get = [pltpu.make_async_copy(src_ref.at[i], buf.at[i], in_s.at[i]) for i in range(count)]
+    put = [pltpu.make_async_copy(buf.at[i], dst_ref.at[i, at], out_s.at[i]) for i in range(count)]
     for copy in get:
         copy.start()
-    for i in range(SHARDS):
+    for i in range(count):
         get[i].wait()
         put[i].start()
     for copy in put:
         copy.wait()
+
+
+def gradients_kernel(src_ref, qkv_ref, out_ref, buf, in_s, out_s):
+    count, slots = 4 * GROUPS, buf.shape[0]
+    get, put = [], []
+    for i in range(count):
+        t, two, slot = i // GROUPS, pl.ds(i % GROUPS * 2, 2), i % slots
+        get.append(pltpu.make_async_copy(src_ref.at[t, two], buf.at[slot], in_s.at[slot]))
+        dst = qkv_ref.at[t, two] if t < 3 else out_ref.at[two]
+        put.append(pltpu.make_async_copy(buf.at[slot], dst, out_s.at[slot]))
+    ahead = slots // 2
+    for copy in get[:ahead]:
+        copy.start()
+    for i in range(count):
+        if i + ahead < count:
+            if i >= ahead:
+                put[i - ahead].wait()
+            get[i + ahead].start()
+        get[i].wait()
+        put[i].start()
+    for copy in put[-2 * ahead:]:
+        copy.wait()
+
+
+def gradients(grads):
+    hbm = pl.BlockSpec(memory_space=pl.ANY)
+    slots = 16
+    return pl.pallas_call(
+        gradients_kernel, in_specs=[hbm], out_specs=[hbm, hbm],
+        out_shape=[jax.ShapeDtypeStruct((3,) + grads.shape[1:], F32), jax.ShapeDtypeStruct(grads.shape[1:], F32)],
+        scratch_shapes=[pltpu.VMEM((slots, 2) + grads.shape[2:], F32), DMA((slots,)), DMA((slots,))], name="gradients",
+        compiler_params=pltpu.CompilerParams(vmem_limit_bytes=48 << 20),
+        cost_estimate=pl.CostEstimate(flops=40_000_000_000, transcendentals=0, bytes_accessed=1 << 27),
+    )(grads)
 
 
 def settle(src, onto=None, rows=RUN):
@@ -763,7 +796,7 @@
     return pl.pallas_call(
         settle_kernel, in_specs=[hbm] * (1 if onto is None else 2), out_specs=hbm,
         out_shape=jax.ShapeDtypeStruct((src.shape[0], rows, src.shape[2]), src.dtype),
-        scratch_shapes=[pltpu.VMEM(src.shape, src.dtype), DMA((SHARDS,)), DMA((SHARDS,))],
+        scratch_shapes=[pltpu.VMEM(src.shape, src.dtype), DMA(src.shape[:1]), DMA(src.shape[:1])],
         input_output_aliases={} if onto is None else {1: 0}, name="settle",
         cost_estimate=pl.CostEstimate(flops=5_000_000_000, transcendentals=0, bytes_accessed=size),
     )(*([src] if onto is None else [src, onto]))
@@ -780,8 +813,9 @@
         grads, y, dx_head, dx_rest, small, *_ = block(x, g, ln_g, ln_b, w_rows, wo, b_qkv, b_out)
         dx_rest = lax.all_to_all(dx_rest, AXES, 0, 0, tiled=True).reshape(SHARDS * BATCH, RUN - DIRECT, MODEL)
         dx = settle(dx_rest, settle(dx_head))
-        d_w_qkv = jnp.transpose(grads[:3].reshape(3, HEADS, HEAD, MODEL), (3, 0, 1, 2))
-        d_w_out = grads[3].reshape(HEADS, HEAD, MODEL)
+        d_w_qkv, d_w_out = gradients(grads)
+        d_w_qkv = jnp.transpose(d_w_qkv.reshape(3, HEADS, HEAD, MODEL), (3, 0, 1, 2))
+        d_w_out = d_w_out.reshape(HEADS, HEAD, MODEL)
         return (settle(y), dx, small[4], small[5], d_w_qkv, small[:3].reshape(3, HEADS, HEAD), d_w_out, small[3])
 
     return jax.shard_map(local_step, mesh=mesh4, in_specs=(tok, tok) + (P(),) * 6,

time: 934 us -> 934 us (level)
  local copies, waits for them, and re-layouts: 47.7 us -> 1.34 us
  Pallas kernels: 878 us -> 923 us
    slice x2 -> x0, local copies, waits for them, and re-layouts: 46.3 us -> none  [the longest x1 34.5 us: local_step(): grads[:3].reshape(3, HEADS, HEAD, MODEL)]
    pallas_call x0 -> x1, Pallas kernels: none -> 43.9 us  [gradients(): pl.pallas_call(gradients_kernel, in_specs=[hbm], out_specs=[hbm, hbm], ou...]
  transfers between devices with their start and end apart: 1 -> 1, of which waited for: 1 -> 1; matrix products, arithmetic and copies ran while one was open for 5% -> 0% of each run, Pallas kernels for 1% -> 6%
where the time goes in v8:
time: 934 us
  Pallas kernels  923 us (99%)
    pallas_call x1, Pallas kernels, block(): pl.pallas_call(block_kernel, grid=(STEPS,), in_specs=[hbm, hbm, vec, vec,...  865 us
    pallas_call x1, Pallas kernels, gradients(): pl.pallas_call(gradients_kernel, in_specs=[hbm], out_specs=[hbm, hbm], ou...  43.9 us
  transfers between devices with their start and end apart: 1, of which 1 were waited for; matrix products, arithmetic and copies ran while one was open for 0% of the time, Pallas kernels for 6%

profile of v8, /device:TPU:0, one launch (start us, length us, event | category | flops | bytes accessed | tf_op | source)
XLA Modules:
  0.0 933.8 jit_solution(11595036971524538762)
XLA Ops:
  0.6 864.6 %block.1 = (f32[4,16,128,2048]{3,2,1,0:T(8,128)}, bf16[16,128,2048]{2,1,0:T(8,128)(2,1)}, bf16[16,48,2048]{2,1,0:T(8,128)(2,1)}, bf16[8,2,80,2048]{3,2,1,0:T(8,1...) custom-call(bf16[16,128,2048]{2,1,0:T(8,128)(2,1)} %x_ref.1, ...), custom_call_target="tpu_custom_call" | custom-call | flops 599999971328 | bytes 209715200 | tf_op jit(solution)/shard_map/block/pallas_call | solution.py:712
  865.2 3.4 all-to-all-start
  868.7 0.0 copy-start
  868.7 6.6 settle.3
  875.3 0.0 copy-done
  875.3 0.7 reshape.50
  876.0 0.6 fusion
  876.6 3.2 settle.4.refs_0_
  879.8 43.9 %gradients.1 = (f32[3,16,128,2048]{3,2,1,0:T(8,128)}, f32[16,128,2048]{2,1,0:T(8,128)}) custom-call(f32[4,16,128,2048]{3,2,1,0:T(8,128)} %get-tuple-element.19.src_ref), custom_call_target="tpu_custom_call" | custom-call | flops 40000000000 | bytes 134217728 | tf_op jit(solution)/shard_map/gradients/pallas_call | solution.py:784
  923.7 5.2 all-to-all-done
  928.9 4.9 settle.5
  (1 shorter events, 0.0 us)
Async XLA Ops:
  865.2 63.7 %all-to-all-start = ((bf16[8,2,80,2048]{3,2,1,0:T(8,128)(2,1)}), bf16[8,2,80,2048]{3,2,1,0:T(8,128)(2,1)}, u32[]{:S(2)}, u32[]{:S(2)}) async-start(bf16[8,2,80,2048]{3,2,1,0:T(8,128)(2,1)} %get-tuple-element.16), calls=%async_computation | async-start | bytes 10485760 | tf_op jit(solution)/shard_map/all_to_all | solution.py:814
  868.7 6.6 copy-start

commit v9 on v7

--- a/solution.py
+++ b/solution.py
@@ -517,9 +517,10 @@
 
     n = j - PAIRS
     k0, k1 = PAIRS - 2, PAIRS - 1
-    for step, ticks in ((2, ((red.scatter2, 0, k1),)), (5, ((red.gather, 0, k1),)),
-                        (7, ((red.scatter2, 1, k1), (red.forward, 1, k0))), (9, ((red.forward, 0, k0),)),
-                        (27, ((red.forward, 0, k1),)), (36, ((red.gather, 1, k1),)), (38, ((red.last, 1, k0),))):
+    for step, ticks in ((1, ((red.forward, 0, k0), (red.forward, 1, k0))),
+                        (2, ((red.scatter2, 0, k1), (red.scatter2, 1, k1))), (5, ((red.gather, 0, k1),)),
+                        (14, ((red.gather, 1, k1),)), (29, ((red.forward, 0, k1),)), (37, ((red.last, 1, k0),)),
+                        (38, ((red.forward, 1, k1),))):
         @pl.when(n == step)
         def _(ticks=ticks):
             for tick, c, k in ticks:
@@ -675,15 +676,14 @@
 
     @pl.when(j == STEPS - 1)
     def _():
-        for tick, c, k in ((red.forward, 1, k1), (red.last, 0, k0), (red.last, 0, k1)):
-            tick(c, k)
+        for c, k in ((1, k1), (0, k0), (0, k1)):
+            red.last(c, k)
         for o in range(1, SHARDS):
             small(o).wait()
         total = smalls[at.slot(0)]
         for r in range(1, SHARDS):
             total += smalls[at.slot(r)]
         sum_ref[...] = total
-        red.last(1, k1)
         for c in range(SPLIT):
             for k in (k0, k1):
                 red.own_sent(c, k)

time: 934 us -> 937 us (level)
  no operation moved by 1% of the time
where the time goes in v9:
time: 937 us; the launch traced here: 936 us
  Pallas kernels  881 us (94%)
  local copies, waits for them, and re-layouts  47.7 us (5%)
    pallas_call x1, Pallas kernels, block(): pl.pallas_call(block_kernel, grid=(STEPS,), in_specs=[hbm, hbm, vec, vec,...  867 us
    slice x1, local copies, waits for them, and re-layouts, local_step(): grads[:3].reshape(3, HEADS, HEAD, MODEL)  34.5 us
  transfers between devices with their start and end apart: 1, of which 1 were waited for; matrix products, arithmetic and copies ran while one was open for 5% of the time, Pallas kernels for 1%

profile of v9, /device:TPU:0, one launch (start us, length us, event | category | flops | bytes accessed | tf_op | source)
XLA Modules:
  0.0 936.4 jit_solution(2693620291741723432)
XLA Ops:
  0.6 867.5 %block.1 = (f32[4,16,128,2048]{3,2,1,0:T(8,128)}, bf16[16,128,2048]{2,1,0:T(8,128)(2,1)}, bf16[16,48,2048]{2,1,0:T(8,128)(2,1)}, bf16[8,2,80,2048]{3,2,1,0:T(8,1...) custom-call(bf16[16,128,2048]{2,1,0:T(8,128)(2,1)} %x_ref.1, ...), custom_call_target="tpu_custom_call" | custom-call | flops 599999971328 | bytes 209715200 | tf_op jit(solution)/shard_map/block/pallas_call | solution.py:712
  868.1 3.4 all-to-all-start
  871.5 11.8 %slice.22 = f32[1,16,128,2048]{3,2,1,0:T(8,128)} slice(f32[4,16,128,2048]{3,2,1,0:T(8,128)} %get-tuple-element.17), slice={[3:4], [0:16], [0:128], [0:2048]} | slice | bytes 33554432 | tf_op jit(solution)/shard_map/slice | solution.py:784
  883.4 0.0 copy-start
  883.4 34.5 %slice.20 = f32[3,16,128,2048]{3,2,1,0:T(8,128)} slice(f32[4,16,128,2048]{3,2,1,0:T(8,128)} %get-tuple-element.17), slice={[0:3], [0:16], [0:128], [0:2048]} | slice | bytes 100663296 | tf_op jit(solution)/shard_map/slice | solution.py:783
  917.9 0.0 copy-done
  917.9 0.7 reshape.47
  918.6 0.6 fusion
  919.2 6.4 settle.3
  925.7 2.8 settle.4.refs_0_
  928.5 3.3 all-to-all-done
  931.8 4.6 settle.5
  (1 shorter events, 0.0 us)
Async XLA Ops:
  868.1 63.7 %all-to-all-start = ((bf16[8,2,80,2048]{3,2,1,0:T(8,128)(2,1)}), bf16[8,2,80,2048]{3,2,1,0:T(8,128)(2,1)}, u32[]{:S(2)}, u32[]{:S(2)}) async-start(bf16[8,2,80,2048]{3,2,1,0:T(8,128)(2,1)} %get-tuple-element.14), calls=%async_computation | async-start | bytes 10485760 | tf_op jit(solution)/shard_map/all_to_all | solution.py:781
  883.4 34.5 %copy-start = (f32[8,2048]{1,0:T(8,128)S(1)}, f32[8,2048]{1,0:T(8,128)}, u32[]{:S(2)}) copy-start(f32[8,2048]{1,0:T(8,128)} %get-tuple-element.16) | copy-start | bytes 196612

commit v10 on v7

--- a/solution.py
+++ b/solution.py
@@ -365,9 +365,17 @@
         project_da(0)
 
     def between(c):
-        @pl.when(j >= 1)
+        @pl.when(j >= 1 + c)
         def _():
             red.scatter2(c, j - 1)
+
+        @pl.when(j == 1)
+        def _():
+            if c == 0:
+                red.scatter2(1, 0)
+            else:
+                red.gather(0, 0)
+                red.gather(1, 0)
 
         if c == 0:
             @pl.when(j >= 2)
@@ -477,7 +485,9 @@
             grad_out(away, c, 1 - at.core)
             meet(c, j).start()
             if c == 0:
-                red.gather(0, j - 1)
+                @pl.when(j >= 2)
+                def _():
+                    red.gather(0, j - 1)
 
         @pl.when(j >= 2)
         def _():
@@ -489,10 +499,9 @@
             grad_qkv(part.at[par], c, at.core)
             grad_out(part.at[par], c, at.core)
             if c == 1:
-                red.gather(1, j - 1)
-
                 @pl.when(j >= 2)
                 def _():
+                    red.gather(1, j - 1)
                     red.last(1, j - 2)
             meet(c, j).wait_recv()
             cols = red.cols(c)

time: 934 us -> 933 us (level)
  no operation moved by 1% of the time
where the time goes in v10:
time: 933 us
  Pallas kernels  878 us (94%)
  local copies, waits for them, and re-layouts  47.7 us (5%)
    pallas_call x1, Pallas kernels, block(): pl.pallas_call(block_kernel, grid=(STEPS,), in_specs=[hbm, hbm, vec, vec,...  864 us
    slice x1, local copies, waits for them, and re-layouts, local_step(): grads[:3].reshape(3, HEADS, HEAD, MODEL)  34.5 us
  transfers between devices with their start and end apart: 1, of which 1 were waited for; matrix products, arithmetic and copies ran while one was open for 5% of the time, Pallas kernels for 1%

profile of v10, /device:TPU:0, one launch (start us, length us, event | category | flops | bytes accessed | tf_op | source)
XLA Modules:
  0.0 932.8 jit_solution(15558107793088294153)
XLA Ops:
  0.6 863.8 %block.1 = (f32[4,16,128,2048]{3,2,1,0:T(8,128)}, bf16[16,128,2048]{2,1,0:T(8,128)(2,1)}, bf16[16,48,2048]{2,1,0:T(8,128)(2,1)}, bf16[8,2,80,2048]{3,2,1,0:T(8,1...) custom-call(bf16[16,128,2048]{2,1,0:T(8,128)(2,1)} %x_ref.1, ...), custom_call_target="tpu_custom_call" | custom-call | flops 599999971328 | bytes 209715200 | tf_op jit(solution)/shard_map/block/pallas_call | solution.py:721
  864.5 3.4 all-to-all-start
  867.9 11.8 %slice.22 = f32[1,16,128,2048]{3,2,1,0:T(8,128)} slice(f32[4,16,128,2048]{3,2,1,0:T(8,128)} %get-tuple-element.17), slice={[3:4], [0:16], [0:128], [0:2048]} | slice | bytes 33554432 | tf_op jit(solution)/shard_map/slice | solution.py:793
  879.7 0.0 copy-start
  879.7 34.5 %slice.20 = f32[3,16,128,2048]{3,2,1,0:T(8,128)} slice(f32[4,16,128,2048]{3,2,1,0:T(8,128)} %get-tuple-element.17), slice={[0:3], [0:16], [0:128], [0:2048]} | slice | bytes 100663296 | tf_op jit(solution)/shard_map/slice | solution.py:792
  914.2 0.0 copy-done
  914.2 0.7 reshape.47
  915.0 0.6 fusion
  915.6 6.4 settle.3
  922.0 2.8 settle.4.refs_0_
  924.8 3.3 all-to-all-done
  928.1 4.6 settle.5
  (1 shorter events, 0.0 us)
Async XLA Ops:
  864.5 63.7 %all-to-all-start = ((bf16[8,2,80,2048]{3,2,1,0:T(8,128)(2,1)}), bf16[8,2,80,2048]{3,2,1,0:T(8,128)(2,1)}, u32[]{:S(2)}, u32[]{:S(2)}) async-start(bf16[8,2,80,2048]{3,2,1,0:T(8,128)(2,1)} %get-tuple-element.14), calls=%async_computation | async-start | bytes 10485760 | tf_op jit(solution)/shard_map/all_to_all | solution.py:790
  879.7 34.5 %copy-start = (f32[8,2048]{1,0:T(8,128)S(1)}, f32[8,2048]{1,0:T(8,128)}, u32[]{:S(2)}) copy-start(f32[8,2048]{1,0:T(8,128)} %get-tuple-element.16) | copy-start | bytes 196612

commit v11 on v10

--- a/solution.py
+++ b/solution.py
@@ -172,7 +172,7 @@
     return r
 
 
-def attend(b, slots, q, k, v, da, a_ref, dq_ref, dk_ref, dv_ref, kt, vt, dk_acc, dv_acc):
+def attend(b, slots, q, k, v, da, a_ref, dq_ref, dk_ref, dv_ref, kt, vt, dk_acc, dv_acc, halfway):
     first = lax.broadcasted_iota(jnp.int32, (SEQ, LANES), 1) < HEAD
     zero = jnp.zeros_like(q)
     qm = (jnp.where(first, q, zero), jnp.where(first, zero, q))
@@ -239,6 +239,8 @@
         if i + 1 < count:
             ready = scores(i + 1)
         outputs(i, pd)
+        if i == 1 and halfway is not None:
+            halfway()
     for r in range(SHARDS):
         run = slice(r * RUN, (r + 1) * RUN)
         dk_ref[slots[r], b] = (dk_acc[run] * scale).astype(BF16)
@@ -346,10 +348,11 @@
         for t in range(2):
             da[t, :, b] = res[:, t * LANES:(t + 1) * LANES].reshape(SHARDS, RUN, LANES)
 
-    def one(b):
+    def one(b, halfway=None):
         gathered = lambda ref, t: jnp.concatenate([ref[t, slots[r], b] for r in range(SHARDS)], axis=0)
         cols = [gathered(qkv, 2 * t + par) for t in range(3)]
-        attend(b, slots, *cols, gathered(da, par), a_ref, dq_ref, dk_ref, dv_ref, kt, vt, dk_acc, dv_acc)
+        attend(b, slots, *cols, gathered(da, par), a_ref, dq_ref, dk_ref, dv_ref, kt, vt, dk_acc, dv_acc,
+               halfway)
 
     @pl.when(j == 0)
     def _():
@@ -374,7 +377,6 @@
             if c == 0:
                 red.scatter2(1, 0)
             else:
-                red.gather(0, 0)
                 red.gather(1, 0)
 
         if c == 0:
@@ -399,7 +401,12 @@
     def _():
         project_da(1)
 
-    one(1)
+    def halfway():
+        @pl.when(j == 1)
+        def _():
+            red.gather(0, 0)
+
+    one(1, halfway)
     between(1)
 
     at_pair = pl.ds(pl.multiple_of(j * LANES, LANES), LANES)

time: 933 us -> 934 us (level)
  no operation moved by 1% of the time
where the time goes in v11:
time: 934 us
  Pallas kernels  878 us (94%)
  local copies, waits for them, and re-layouts  47.7 us (5%)
    pallas_call x1, Pallas kernels, block(): pl.pallas_call(block_kernel, grid=(STEPS,), in_specs=[hbm, hbm, vec, vec,...  864 us
    slice x1, local copies, waits for them, and re-layouts, local_step(): grads[:3].reshape(3, HEADS, HEAD, MODEL)  34.5 us
  transfers between devices with their start and end apart: 1, of which 1 were waited for; matrix products, arithmetic and copies ran while one was open for 5% of the time, Pallas kernels for 1%

profile of v11, /device:TPU:0, one launch (start us, length us, event | category | flops | bytes accessed | tf_op | source)
XLA Modules:
  0.0 933.7 jit_solution(7758362450500637417)
XLA Ops:
  0.6 864.5 %block.1 = (f32[4,16,128,2048]{3,2,1,0:T(8,128)}, bf16[16,128,2048]{2,1,0:T(8,128)(2,1)}, bf16[16,48,2048]{2,1,0:T(8,128)(2,1)}, bf16[8,2,80,2048]{3,2,1,0:T(8,1...) custom-call(bf16[16,128,2048]{2,1,0:T(8,128)(2,1)} %x_ref.1, ...), custom_call_target="tpu_custom_call" | custom-call | flops 599999971328 | bytes 209715200 | tf_op jit(solution)/shard_map/block/pallas_call | solution.py:728
  865.1 3.7 all-to-all-start
  868.8 11.8 %slice.22 = f32[1,16,128,2048]{3,2,1,0:T(8,128)} slice(f32[4,16,128,2048]{3,2,1,0:T(8,128)} %get-tuple-element.17), slice={[3:4], [0:16], [0:128], [0:2048]} | slice | bytes 33554432 | tf_op jit(solution)/shard_map/slice | solution.py:800
  880.6 0.0 copy-start
  880.6 34.5 %slice.20 = f32[3,16,128,2048]{3,2,1,0:T(8,128)} slice(f32[4,16,128,2048]{3,2,1,0:T(8,128)} %get-tuple-element.17), slice={[0:3], [0:16], [0:128], [0:2048]} | slice | bytes 100663296 | tf_op jit(solution)/shard_map/slice | solution.py:799
  915.1 0.0 copy-done
  915.1 0.7 reshape.47
  915.8 0.6 fusion
  916.5 6.4 settle.3
  922.9 2.8 settle.4.refs_0_
  925.7 3.4 all-to-all-done
  929.1 4.6 settle.5
  (1 shorter events, 0.0 us)
Async XLA Ops:
  865.1 64.0 %all-to-all-start = ((bf16[8,2,80,2048]{3,2,1,0:T(8,128)(2,1)}), bf16[8,2,80,2048]{3,2,1,0:T(8,128)(2,1)}, u32[]{:S(2)}, u32[]{:S(2)}) async-start(bf16[8,2,80,2048]{3,2,1,0:T(8,128)(2,1)} %get-tuple-element.14), calls=%async_computation | async-start | bytes 10485760 | tf_op jit(solution)/shard_map/all_to_all | solution.py:797
  880.6 34.5 %copy-start = (f32[8,2048]{1,0:T(8,128)S(1)}, f32[8,2048]{1,0:T(8,128)}, u32[]{:S(2)}) copy-start(f32[8,2048]{1,0:T(8,128)} %get-tuple-element.16) | copy-start | bytes 196612
